TPU v7x, 32 devices: a whole 2x2x4 slice. The times are simulated.
32 devices in a mesh: mission: 2 (over x), arc: 16 (over z, y, core).
Axes of the slice: x: 2, y: 2, z: 4, core: 2. Of those that a mesh axis runs over, the one named last changes fastest.
Arguments:
- design: bfloat16 [2560, 5120], P(('mission', 'arc')), may hold values from -3 to 3
- nuisance_design: bfloat16 [2560, 128], P(('mission', 'arc')), may hold values from -1 to 1
- observed: float32 [2560], P(('mission', 'arc')), may hold values from -6 to 6
- arc_of_row: int32 [2560], P(('mission', 'arc')), may hold values from 0 to 1, as said below
- nuis_size: int32 [64], P(('mission', 'arc')), may hold values from 32 to 128
- weight_index: int32 [2560], P(('mission', 'arc')), may hold values from 0 to 7
- kind_weight: float32 [8], replicated, may hold values from 0.3 to 3
- mission_weight: float32 [2], P('mission'), may hold values from 0.3 to 3
Outputs:
- normal_fold: float32 [2560, 5120], P(('mission', 'arc'))
- right_side: float32 [5120], P(('mission', 'arc'))
- tail_diagonal: float32 [2560], P(('mission', 'arc'))
Inputs may be any that keep to these rules, and one draw needn't show every extreme that they name: `arc_of_row`: in each row block of 80 rows the rows of arc 0 come first and those of arc 1 follow; each arc has at least 20 rows.
All inputs are finite; a program needn't handle non-finite values.
Results may differ from a plain program's by a relative error of at most 0.019.
Values may be sent and summed in bfloat16 or wider, within the bound.
A program may use at most 192 MiB of HBM per device.

v0:
```python
import jax
import jax.numpy as jnp
from jax import lax
from jax.sharding import PartitionSpec as P

ARCS_DEV = 2


def local_system(
    design, nuisance_design, observed, arc_of_row, nuis_size, weight_index, kind_weight
):
    kind_ids = jnp.arange(kind_weight.shape[0], dtype=jnp.int32)
    row_weight = jnp.sum(
        jnp.where(weight_index[:, None] == kind_ids[None, :], kind_weight[None, :], 0.0), axis=1
    )
    nuis_ids = jnp.arange(nuisance_design.shape[1], dtype=jnp.int32)
    eye_block = jnp.eye(nuisance_design.shape[1], dtype=jnp.float32)
    blocks = []
    solved = []
    solved_obs = []
    for arc_id in range(ARCS_DEV):
        col_mask = (nuis_ids < nuis_size[arc_id]).astype(jnp.bfloat16)
        in_arc = (arc_of_row == arc_id).astype(jnp.float32)
        masked = nuisance_design * col_mask[None, :]
        weighted = (masked.astype(jnp.float32) * (row_weight * in_arc)[:, None]).astype(
            jnp.bfloat16
        )
        normal_ll = jnp.dot(weighted.T, masked, preferred_element_type=jnp.float32) + eye_block
        coupling = jnp.dot(weighted.T, design, preferred_element_type=jnp.float32)
        obs_part = jnp.dot(
            weighted.T.astype(jnp.float32), observed, precision=lax.Precision.HIGHEST
        )
        factor = jnp.linalg.cholesky(normal_ll)
        blocks.append(weighted)
        solved.append(jax.scipy.linalg.cho_solve((factor, True), coupling).astype(jnp.bfloat16))
        solved_obs.append(jax.scipy.linalg.cho_solve((factor, True), obs_part))
    stacked = jnp.concatenate(blocks, axis=1)
    solved_all = jnp.concatenate(solved, axis=0)
    obs_all = jnp.concatenate(solved_obs, axis=0)
    reduced = (
        row_weight[:, None] * design.astype(jnp.float32)
        - jnp.dot(stacked, solved_all, preferred_element_type=jnp.float32)
    ).astype(jnp.bfloat16)
    reduced_obs = (
        row_weight * observed
        - jnp.dot(stacked.astype(jnp.float32), obs_all, precision=lax.Precision.HIGHEST)
    ).astype(jnp.bfloat16)
    right_term = jnp.dot(reduced_obs, design, preferred_element_type=jnp.float32)
    half_width = design.shape[1] // 2
    tail_term = jnp.sum(
        design[:, half_width:].astype(jnp.float32) * reduced[:, half_width:].astype(jnp.float32),
        axis=0,
    )
    return (reduced, right_term, tail_term)


def on_device(
    design,
    nuisance_design,
    observed,
    arc_of_row,
    nuis_size,
    weight_index,
    kind_weight,
    mission_weight,
):
    reduced, right_term, tail_term = local_system(
        design, nuisance_design, observed, arc_of_row, nuis_size, weight_index, kind_weight
    )
    weight = mission_weight[0]
    width_all = design.shape[1]
    half_width = width_all // 2
    groups = lax.axis_size("mission")
    members = lax.axis_size("arc")
    final_rows = half_width // (groups * members)
    mirrored = design[:, ::-1]
    reduced_mirror = reduced[:, ::-1]
    row_numbers = jnp.arange(half_width, dtype=jnp.int32)

    def permute(matrix):
        shaped = matrix.reshape(matrix.shape[0], groups, members, final_rows)
        return jnp.transpose(shaped, (0, 2, 1, 3)).reshape(matrix.shape[0], half_width)

    cols_above = permute(design[:, :half_width])
    cols_mirror = permute(mirrored[:, :half_width])
    row_order = permute(row_numbers[None, :])[0]
    columns = jnp.arange(width_all, dtype=jnp.int32)
    contract_dims = (((0,), (0,)), ((), ()))
    tile_cols = 512
    tile_count = width_all // tile_cols

    def fold_rows():
        block_rows = lax.axis_size("arc") * (half_width // members)
        while block_rows > 640 and block_rows % 2 == 0:
            block_rows = block_rows // 2

        def one_block(block_id):
            block_start = block_id * block_rows
            above_cols = lax.dynamic_slice_in_dim(cols_above, block_start, block_rows, 1)
            mirror_cols = lax.dynamic_slice_in_dim(cols_mirror, block_start, block_rows, 1)
            rows_here = lax.dynamic_slice_in_dim(row_order, block_start, block_rows, 0)
            low_row = jnp.min(rows_here)
            high_row = jnp.max(rows_here)
            pieces = []
            for tile_id in range(tile_count):
                col_start = tile_id * tile_cols
                above_tile = reduced[:, col_start : col_start + tile_cols]
                mirror_tile = reduced_mirror[:, col_start : col_start + tile_cols]
                tile_ids = columns[col_start : col_start + tile_cols]

                def above_only():
                    return lax.dot_general(
                        above_cols, above_tile, contract_dims, preferred_element_type=jnp.float32
                    )

                def mirror_only():
                    return lax.dot_general(
                        mirror_cols, mirror_tile, contract_dims, preferred_element_type=jnp.float32
                    )

                def mixed_tile():
                    return jnp.where(
                        tile_ids[None, :] >= rows_here[:, None], above_only(), mirror_only()
                    )

                tile_kind = jnp.where(
                    col_start >= high_row, 0, jnp.where(col_start + tile_cols <= low_row, 1, 2)
                ).astype(jnp.int32)
                pieces.append(lax.switch(tile_kind, [above_only, mirror_only, mixed_tile]))
            return weight * jnp.concatenate(pieces, axis=1)

        stacked_pieces = lax.map(
            one_block,
            jnp.arange(
                lax.axis_size("arc") * (half_width // members) // block_rows, dtype=jnp.int32
            ),
        )
        return stacked_pieces.reshape(lax.axis_size("arc") * (half_width // members), width_all)

    partial_fold = lax.psum_scatter(
        fold_rows().astype(jnp.bfloat16), "arc", scatter_dimension=0, tiled=True
    )
    normal_fold = lax.psum_scatter(partial_fold, "mission", scatter_dimension=0, tiled=True).astype(
        jnp.float32
    )
    right_side, tail_diagonal = (
        lax.psum_scatter(weight * right_term, ("mission", "arc"), scatter_dimension=0, tiled=True),
        lax.psum_scatter(weight * tail_term, ("mission", "arc"), scatter_dimension=0, tiled=True),
    )
    return (normal_fold, right_side, tail_diagonal)


def solution(mesh):
    placed = (
        P(("mission", "arc"), None),
        P(("mission", "arc"), None),
        P(("mission", "arc")),
        P(("mission", "arc")),
        P(("mission", "arc")),
        P(("mission", "arc")),
        P(),
        P("mission"),
    )
    return jax.shard_map(
        on_device,
        mesh=mesh,
        in_specs=placed,
        out_specs=(P(("mission", "arc"), None), P(("mission", "arc")), P(("mission", "arc"))),
        check_vma=False,
    )
```

profile of v0, /device:TPU:0, one launch (start us, length us, event | category | flops | bytes accessed | tf_op | source)
XLA Modules:
  0.0 654.3 jit_solution(15927628638718782707)
XLA Ops:
  19.8 11.7 %cholesky.44 = f32[128,128]{1,0:T(8,128)S(1)} custom-call(f32[128,128]{1,0:T(8,128)S(1)} %fusion.32), custom_call_target="Cholesky" | custom-call | tf_op jit(solution)/shard_map/jit(cholesky)/cholesky | solution.py:33
  32.9 9.8 %custom-call.14 = f32[1,128,128]{1,2,0:T(8,128)S(1)} custom-call(f32[1,128,128]{2,1,0:T(8,128)S(1)} %fusion.19), custom_call_target="InvertDiagBlocksLowerTriangular" | custom-call | tf_op jit(solution)/shard_map/jit(_cho_solve)/triangular_solve | solution.py:35
  42.8 11.7 %cholesky.55 = f32[128,128]{1,0:T(8,128)S(1)} custom-call(f32[128,128]{1,0:T(8,128)S(1)} %fusion.26), custom_call_target="Cholesky" | custom-call | tf_op jit(solution)/shard_map/jit(cholesky)/cholesky | solution.py:33
  55.9 20.9 %custom-call.15 = f32[1,128,128]{1,2,0:T(8,128)S(1)} custom-call(f32[1,128,128]{2,1,0:T(8,128)S(1)} %fusion.20), custom_call_target="InvertDiagBlocksLowerTriangular" | custom-call | tf_op jit(solution)/shard_map/jit(_cho_solve)/triangular_solve | solution.py:35
  83.6 4.2 fusion.30
  87.8 2.4 convolution_convert_fusion.1
  90.2 2.5 fusion.24
  92.6 2.4 convolution_convert_fusion
  95.7 3.7 rev.4
  99.3 247.2 %while.12 = (s32[]{:T(128)}, bf16[4,640,5120]{2,1,0:T(8,128)(2,1)}, f32[]{:T(128)}, s32[4]{0:T(128)S(1)}, s32[2560]{0:T(1024)S(1)}, /*index=5*/bf16[80,2560]{1,0...) while((s32[]{:T(128)}, bf16[4,640,5120]{2,1,0:T(8,128)(2,1)}, ...), condition=%wide.region_36.39_spmd.clone.clone, body=%wide.region_3.38_spmd.clone.clone.sunk | while | flops 1058407680 | bytes 157238096 | solution.py:132
  117.9 2.3 conditional.47
  117.9 2.3 convolution_bitcast_fusion.14
  120.2 2.3 conditional.46
  120.2 2.3 convolution_bitcast_fusion.12
  122.6 2.3 conditional.45
  122.6 2.3 convolution_bitcast_fusion.10
  124.9 2.3 conditional.44
  134.3 2.6 constant_dynamic-update-slice_fusion.20
  151.4 9.8 %multiply_dynamic-update-slice_fusion.2 = bf16[4,640,5120]{2,1,0:T(8,128)(2,1)} fusion(bf16[4,640,5120]{2,1,0:T(8,128)(2,1)} %get-tuple-element.682, s32[]{:T(128)S(6)} %copy.81, f32[1,640,5120]{2,1,0:T(8,128)} %constant_dynamic-update-slice_fusion.29, f32[]{:T(128)} %get-tuple-element.706), kind=kLoop, calls=%fused_computation.41.clone.1 | loop fusion | flops 3276800 | bytes 26214916 | tf_op jit(solution)/shard_map/while/body/jit(dynamic_update_index_in_dim)/dynamic_update_slice | solution.py:132
  179.7 2.3 conditional.47
  179.7 2.3 convolution_bitcast_fusion.14
  182.0 2.3 conditional.46
  182.0 2.3 convolution_bitcast_fusion.12
  184.3 2.3 conditional.45
  184.3 2.3 convolution_bitcast_fusion.10
  196.1 2.6 constant_dynamic-update-slice_fusion.20
  213.2 9.9 %multiply_dynamic-update-slice_fusion.2 = bf16[4,640,5120]{2,1,0:T(8,128)(2,1)} fusion(bf16[4,640,5120]{2,1,0:T(8,128)(2,1)} %get-tuple-element.682, s32[]{:T(128)S(6)} %copy.81, f32[1,640,5120]{2,1,0:T(8,128)} %constant_dynamic-update-slice_fusion.29, f32[]{:T(128)} %get-tuple-element.706), kind=kLoop, calls=%fused_computation.41.clone.1 | loop fusion | flops 3276800 | bytes 26214916 | tf_op jit(solution)/shard_map/while/body/jit(dynamic_update_index_in_dim)/dynamic_update_slice | solution.py:132
  241.5 2.3 conditional.47
  241.5 2.3 convolution_bitcast_fusion.14
  243.8 2.3 conditional.46
  243.8 2.3 convolution_bitcast_fusion.12
  246.1 2.3 conditional.45
  246.1 2.3 convolution_bitcast_fusion.10
  248.4 2.7 conditional.44
  257.9 2.6 constant_dynamic-update-slice_fusion.20
  275.0 9.8 %multiply_dynamic-update-slice_fusion.2 = bf16[4,640,5120]{2,1,0:T(8,128)(2,1)} fusion(bf16[4,640,5120]{2,1,0:T(8,128)(2,1)} %get-tuple-element.682, s32[]{:T(128)S(6)} %copy.81, f32[1,640,5120]{2,1,0:T(8,128)} %constant_dynamic-update-slice_fusion.29, f32[]{:T(128)} %get-tuple-element.706), kind=kLoop, calls=%fused_computation.41.clone.1 | loop fusion | flops 3276800 | bytes 26214916 | tf_op jit(solution)/shard_map/while/body/jit(dynamic_update_index_in_dim)/dynamic_update_slice | solution.py:132
  303.2 2.3 conditional.47
  303.2 2.3 convolution_bitcast_fusion.14
  305.5 2.3 conditional.46
  305.5 2.3 convolution_bitcast_fusion.12
  307.8 2.3 conditional.45
  307.8 2.3 convolution_bitcast_fusion.10
  310.1 2.7 conditional.44
  319.6 2.6 constant_dynamic-update-slice_fusion.20
  336.7 9.8 %multiply_dynamic-update-slice_fusion.2 = bf16[4,640,5120]{2,1,0:T(8,128)(2,1)} fusion(bf16[4,640,5120]{2,1,0:T(8,128)(2,1)} %get-tuple-element.682, s32[]{:T(128)S(6)} %copy.81, f32[1,640,5120]{2,1,0:T(8,128)} %constant_dynamic-update-slice_fusion.29, f32[]{:T(128)} %get-tuple-element.706), kind=kLoop, calls=%fused_computation.41.clone.1 | loop fusion | flops 3276800 | bytes 26214916 | tf_op jit(solution)/shard_map/while/body/jit(dynamic_update_index_in_dim)/dynamic_update_slice | solution.py:132
  346.8 254.0 %reduce-scatter.3.cloned.1.call-done = bf16[160,5120]{1,0:T(8,128)(2,1)} async-done(((bf16[2560,5120]{1,0:T(8,128)(2,1)}), bf16[160,5120]{1,0:T(8,128)(2,1)}) %reduce-scatter.3.cloned.1.call-update) | async-done | bytes 1638416 | tf_op jit(solution)/shard_map/reduce_scatter | solution.py:140
  603.3 40.1 %all-reduce.2 = (f32[5120]{0:T(1024)S(1)}, f32[2560]{0:T(1024)S(1)}) all-reduce(f32[5120]{0:T(1024)S(1)} %broadcast_multiply_fusion, f32[2560]{0:T(1024)S(1)} %broadcast_multiply_fusion.1), channel_id=4, replica_groups=mesh['mission'=2,'arc'=16] {'mission','arc'}, use_global_device_ids=true, to_apply=%region_39.43.clone | all-reduce | flops 7680 | bytes 61440
  644.6 2.4 convert_element_type.79
  (368 shorter events, 176.4 us)
Async XLA Ops:
  7.2 593.6 %reduce-scatter.3.cloned.1.call-start = ((), (), s32[]{:S(2)}) async-start(), calls=%async_computation.2 | async-start | bytes 27852800 | tf_op jit(solution)/shard_map/reduce_scatter | solution.py:140
  9.3 85.7 %copy-start.41 = (f32[80]{0:T(128)}, f32[80]{0:T(128)S(1)}, u32[]{:S(2)}) copy-start(f32[80]{0:T(128)S(1)} %select_reduce_fusion.2) | copy-start | bytes 964
  13.2 81.8 %copy-start.29 = (bf16[80,128]{1,0:T(8,128)(2,1)}, bf16[80,128]{1,0:T(8,128)(2,1)S(1)}, u32[]{:S(2)}) copy-start(bf16[80,128]{1,0:T(8,128)(2,1)S(1)} %get-tuple-element.545) | copy-start | bytes 61444
  13.2 81.8 %copy-start.31 = (bf16[80,128]{1,0:T(8,128)(2,1)}, bf16[80,128]{1,0:T(8,128)(2,1)S(1)}, u32[]{:S(2)}) copy-start(bf16[80,128]{1,0:T(8,128)(2,1)S(1)} %get-tuple-element.546) | copy-start | bytes 61444
  42.7 45.0 %copy-start.23 = (f32[1,128,128]{1,2,0:T(8,128)}, f32[1,128,128]{1,2,0:T(8,128)S(1)}, u32[]{:S(2)}) copy-start(f32[1,128,128]{1,2,0:T(8,128)S(1)} %custom-call.14) | copy-start | bytes 196612
  76.8 15.8 %copy-start.25 = (f32[1,128,128]{1,2,0:T(8,128)}, f32[1,128,128]{1,2,0:T(8,128)S(1)}, u32[]{:S(2)}) copy-start(f32[1,128,128]{1,2,0:T(8,128)S(1)} %custom-call.15) | copy-start | bytes 196612
  99.5 15.2 %copy-start.19 = (bf16[80,2560]{1,0:T(8,128)(2,1)}, bf16[80,2560]{1,0:T(8,128)(2,1)S(1)}, u32[]{:S(2)}) copy-start(bf16[80,2560]{1,0:T(8,128)(2,1)S(1)} %get-tuple-element.711) | copy-start | bytes 1228804 | tf_op jit(solution)/shard_map/while
  99.6 15.2 %copy-start.21 = (bf16[80,2560]{1,0:T(8,128)(2,1)}, bf16[80,2560]{1,0:T(8,128)(2,1)S(1)}, u32[]{:S(2)}) copy-start(bf16[80,2560]{1,0:T(8,128)(2,1)S(1)} %get-tuple-element.709) | copy-start | bytes 1228804 | tf_op jit(solution)/shard_map/while
  99.6 16.7 %copy-start.7 = (bf16[80,5120]{1,0:T(8,128)(2,1)}, bf16[80,5120]{1,0:T(8,128)(2,1)S(1)}, u32[]{:S(2)}) copy-start(bf16[80,5120]{1,0:T(8,128)(2,1)S(1)} %get-tuple-element.710) | copy-start | bytes 2457604 | tf_op jit(solution)/shard_map/while
  99.6 16.7 %copy-start.9 = (bf16[80,5120]{1,0:T(8,128)(2,1)}, bf16[80,5120]{1,0:T(8,128)(2,1)S(1)}, u32[]{:S(2)}) copy-start(bf16[80,5120]{1,0:T(8,128)(2,1)S(1)} %get-tuple-element.712) | copy-start | bytes 2457604 | tf_op jit(solution)/shard_map/while
  151.4 9.9 %copy-start.8 = (bf16[80,5120]{1,0:T(8,128)(2,1)S(1)}, bf16[80,5120]{1,0:T(8,128)(2,1)}, u32[]{:S(2)}) copy-start(bf16[80,5120]{1,0:T(8,128)(2,1)} %copy-done.7) | copy-start | bytes 2457604 | tf_op jit(solution)/shard_map/while
  151.4 9.9 %copy-start.10 = (bf16[80,5120]{1,0:T(8,128)(2,1)S(1)}, bf16[80,5120]{1,0:T(8,128)(2,1)}, u32[]{:S(2)}) copy-start(bf16[80,5120]{1,0:T(8,128)(2,1)} %copy-done.9) | copy-start | bytes 2457604 | tf_op jit(solution)/shard_map/while
  151.4 9.9 %copy-start.20 = (bf16[80,2560]{1,0:T(8,128)(2,1)S(1)}, bf16[80,2560]{1,0:T(8,128)(2,1)}, u32[]{:S(2)}) copy-start(bf16[80,2560]{1,0:T(8,128)(2,1)} %copy-done.19) | copy-start | bytes 1228804 | tf_op jit(solution)/shard_map/while
  151.4 9.9 %copy-start.22 = (bf16[80,2560]{1,0:T(8,128)(2,1)S(1)}, bf16[80,2560]{1,0:T(8,128)(2,1)}, u32[]{:S(2)}) copy-start(bf16[80,2560]{1,0:T(8,128)(2,1)} %copy-done.21) | copy-start | bytes 1228804 | tf_op jit(solution)/shard_map/while
  161.3 15.2 %copy-start.19 = (bf16[80,2560]{1,0:T(8,128)(2,1)}, bf16[80,2560]{1,0:T(8,128)(2,1)S(1)}, u32[]{:S(2)}) copy-start(bf16[80,2560]{1,0:T(8,128)(2,1)S(1)} %get-tuple-element.711) | copy-start | bytes 1228804 | tf_op jit(solution)/shard_map/while
  161.3 15.2 %copy-start.21 = (bf16[80,2560]{1,0:T(8,128)(2,1)}, bf16[80,2560]{1,0:T(8,128)(2,1)S(1)}, u32[]{:S(2)}) copy-start(bf16[80,2560]{1,0:T(8,128)(2,1)S(1)} %get-tuple-element.709) | copy-start | bytes 1228804 | tf_op jit(solution)/shard_map/while
  161.3 16.7 %copy-start.7 = (bf16[80,5120]{1,0:T(8,128)(2,1)}, bf16[80,5120]{1,0:T(8,128)(2,1)S(1)}, u32[]{:S(2)}) copy-start(bf16[80,5120]{1,0:T(8,128)(2,1)S(1)} %get-tuple-element.710) | copy-start | bytes 2457604 | tf_op jit(solution)/shard_map/while
  161.3 16.7 %copy-start.9 = (bf16[80,5120]{1,0:T(8,128)(2,1)}, bf16[80,5120]{1,0:T(8,128)(2,1)S(1)}, u32[]{:S(2)}) copy-start(bf16[80,5120]{1,0:T(8,128)(2,1)S(1)} %get-tuple-element.712) | copy-start | bytes 2457604 | tf_op jit(solution)/shard_map/while
  213.1 9.9 %copy-start.8 = (bf16[80,5120]{1,0:T(8,128)(2,1)S(1)}, bf16[80,5120]{1,0:T(8,128)(2,1)}, u32[]{:S(2)}) copy-start(bf16[80,5120]{1,0:T(8,128)(2,1)} %copy-done.7) | copy-start | bytes 2457604 | tf_op jit(solution)/shard_map/while
  213.1 9.9 %copy-start.10 = (bf16[80,5120]{1,0:T(8,128)(2,1)S(1)}, bf16[80,5120]{1,0:T(8,128)(2,1)}, u32[]{:S(2)}) copy-start(bf16[80,5120]{1,0:T(8,128)(2,1)} %copy-done.9) | copy-start | bytes 2457604 | tf_op jit(solution)/shard_map/while
  213.1 9.9 %copy-start.20 = (bf16[80,2560]{1,0:T(8,128)(2,1)S(1)}, bf16[80,2560]{1,0:T(8,128)(2,1)}, u32[]{:S(2)}) copy-start(bf16[80,2560]{1,0:T(8,128)(2,1)} %copy-done.19) | copy-start | bytes 1228804 | tf_op jit(solution)/shard_map/while
  213.1 9.9 %copy-start.22 = (bf16[80,2560]{1,0:T(8,128)(2,1)S(1)}, bf16[80,2560]{1,0:T(8,128)(2,1)}, u32[]{:S(2)}) copy-start(bf16[80,2560]{1,0:T(8,128)(2,1)} %copy-done.21) | copy-start | bytes 1228804 | tf_op jit(solution)/shard_map/while
  223.1 15.2 %copy-start.19 = (bf16[80,2560]{1,0:T(8,128)(2,1)}, bf16[80,2560]{1,0:T(8,128)(2,1)S(1)}, u32[]{:S(2)}) copy-start(bf16[80,2560]{1,0:T(8,128)(2,1)S(1)} %get-tuple-element.711) | copy-start | bytes 1228804 | tf_op jit(solution)/shard_map/while
  223.1 15.2 %copy-start.21 = (bf16[80,2560]{1,0:T(8,128)(2,1)}, bf16[80,2560]{1,0:T(8,128)(2,1)S(1)}, u32[]{:S(2)}) copy-start(bf16[80,2560]{1,0:T(8,128)(2,1)S(1)} %get-tuple-element.709) | copy-start | bytes 1228804 | tf_op jit(solution)/shard_map/while
  223.1 16.7 %copy-start.7 = (bf16[80,5120]{1,0:T(8,128)(2,1)}, bf16[80,5120]{1,0:T(8,128)(2,1)S(1)}, u32[]{:S(2)}) copy-start(bf16[80,5120]{1,0:T(8,128)(2,1)S(1)} %get-tuple-element.710) | copy-start | bytes 2457604 | tf_op jit(solution)/shard_map/while
  223.1 16.7 %copy-start.9 = (bf16[80,5120]{1,0:T(8,128)(2,1)}, bf16[80,5120]{1,0:T(8,128)(2,1)S(1)}, u32[]{:S(2)}) copy-start(bf16[80,5120]{1,0:T(8,128)(2,1)S(1)} %get-tuple-element.712) | copy-start | bytes 2457604 | tf_op jit(solution)/shard_map/while
  275.0 9.8 %copy-start.22 = (bf16[80,2560]{1,0:T(8,128)(2,1)S(1)}, bf16[80,2560]{1,0:T(8,128)(2,1)}, u32[]{:S(2)}) copy-start(bf16[80,2560]{1,0:T(8,128)(2,1)} %copy-done.21) | copy-start | bytes 1228804 | tf_op jit(solution)/shard_map/while
  284.8 15.2 %copy-start.19 = (bf16[80,2560]{1,0:T(8,128)(2,1)}, bf16[80,2560]{1,0:T(8,128)(2,1)S(1)}, u32[]{:S(2)}) copy-start(bf16[80,2560]{1,0:T(8,128)(2,1)S(1)} %get-tuple-element.711) | copy-start | bytes 1228804 | tf_op jit(solution)/shard_map/while
  284.8 15.2 %copy-start.21 = (bf16[80,2560]{1,0:T(8,128)(2,1)}, bf16[80,2560]{1,0:T(8,128)(2,1)S(1)}, u32[]{:S(2)}) copy-start(bf16[80,2560]{1,0:T(8,128)(2,1)S(1)} %get-tuple-element.709) | copy-start | bytes 1228804 | tf_op jit(solution)/shard_map/while
  284.8 16.7 %copy-start.7 = (bf16[80,5120]{1,0:T(8,128)(2,1)}, bf16[80,5120]{1,0:T(8,128)(2,1)S(1)}, u32[]{:S(2)}) copy-start(bf16[80,5120]{1,0:T(8,128)(2,1)S(1)} %get-tuple-element.710) | copy-start | bytes 2457604 | tf_op jit(solution)/shard_map/while
  284.8 16.7 %copy-start.9 = (bf16[80,5120]{1,0:T(8,128)(2,1)}, bf16[80,5120]{1,0:T(8,128)(2,1)S(1)}, u32[]{:S(2)}) copy-start(bf16[80,5120]{1,0:T(8,128)(2,1)S(1)} %get-tuple-element.712) | copy-start | bytes 2457604 | tf_op jit(solution)/shard_map/while
  336.7 9.8 %copy-start.8 = (bf16[80,5120]{1,0:T(8,128)(2,1)S(1)}, bf16[80,5120]{1,0:T(8,128)(2,1)}, u32[]{:S(2)}) copy-start(bf16[80,5120]{1,0:T(8,128)(2,1)} %copy-done.7) | copy-start | bytes 2457604 | tf_op jit(solution)/shard_map/while
  336.7 9.8 %copy-start.10 = (bf16[80,5120]{1,0:T(8,128)(2,1)S(1)}, bf16[80,5120]{1,0:T(8,128)(2,1)}, u32[]{:S(2)}) copy-start(bf16[80,5120]{1,0:T(8,128)(2,1)} %copy-done.9) | copy-start | bytes 2457604 | tf_op jit(solution)/shard_map/while
  336.7 9.8 %copy-start.20 = (bf16[80,2560]{1,0:T(8,128)(2,1)S(1)}, bf16[80,2560]{1,0:T(8,128)(2,1)}, u32[]{:S(2)}) copy-start(bf16[80,2560]{1,0:T(8,128)(2,1)} %copy-done.19) | copy-start | bytes 1228804 | tf_op jit(solution)/shard_map/while
  336.7 9.9 %copy-start.22 = (bf16[80,2560]{1,0:T(8,128)(2,1)S(1)}, bf16[80,2560]{1,0:T(8,128)(2,1)}, u32[]{:S(2)}) copy-start(bf16[80,2560]{1,0:T(8,128)(2,1)} %copy-done.21) | copy-start | bytes 1228804 | tf_op jit(solution)/shard_map/while
  346.6 254.8 %copy-start.28 = (bf16[80,128]{1,0:T(8,128)(2,1)S(1)}, bf16[80,128]{1,0:T(8,128)(2,1)}, u32[]{:S(2)}) copy-start(bf16[80,128]{1,0:T(8,128)(2,1)} %param.46) | copy-start | bytes 61444
  346.6 254.8 %copy-start.38 = (f32[80]{0:T(128)S(1)}, f32[80]{0:T(128)}, u32[]{:S(2)}) copy-start(f32[80]{0:T(128)} %copy-done.37) | copy-start | bytes 964
  346.6 254.8 %copy-start.40 = (bf16[128]{0:T(256)(128)(2,1)S(1)}, bf16[128]{0:T(256)(128)(2,1)}, u32[]{:S(2)}) copy-start(bf16[128]{0:T(256)(128)(2,1)} %copy-done.39) | copy-start | bytes 772
  346.6 254.8 %copy-start.43 = (f32[80]{0:T(128)S(1)}, f32[80]{0:T(128)}, u32[]{:S(2)}) copy-start(f32[80]{0:T(128)} %param.47) | copy-start | bytes 964
  346.6 255.0 %copy-start.24 = (f32[1,128,128]{1,2,0:T(8,128)S(1)}, f32[1,128,128]{1,2,0:T(8,128)}, u32[]{:S(2)}) copy-start(f32[1,128,128]{1,2,0:T(8,128)} %copy-done.23) | copy-start | bytes 196612
  346.6 255.4 %copy-start.34 = (f32[80]{0:T(128)S(1)}, f32[80]{0:T(128)}, u32[]{:S(2)}) copy-start(f32[80]{0:T(128)} %copy-done.33) | copy-start | bytes 964
  346.7 255.4 %copy-start.36 = (bf16[128]{0:T(256)(128)(2,1)S(1)}, bf16[128]{0:T(256)(128)(2,1)}, u32[]{:S(2)}) copy-start(bf16[128]{0:T(256)(128)(2,1)} %copy-done.35) | copy-start | bytes 772
  346.7 255.6 %copy-start.26 = (f32[1,128,128]{1,2,0:T(8,128)S(1)}, f32[1,128,128]{1,2,0:T(8,128)}, u32[]{:S(2)}) copy-start(f32[1,128,128]{1,2,0:T(8,128)} %copy-done.25) | copy-start | bytes 196612
  346.7 256.0 %copy-start.30 = (bf16[80,128]{1,0:T(8,128)(2,1)S(1)}, bf16[80,128]{1,0:T(8,128)(2,1)}, u32[]{:S(2)}) copy-start(bf16[80,128]{1,0:T(8,128)(2,1)} %copy-done.29) | copy-start | bytes 61444
  346.7 256.0 %copy-start.32 = (bf16[80,128]{1,0:T(8,128)(2,1)S(1)}, bf16[80,128]{1,0:T(8,128)(2,1)}, u32[]{:S(2)}) copy-start(bf16[80,128]{1,0:T(8,128)(2,1)} %copy-done.31) | copy-start | bytes 61444
  346.7 256.0 %copy-start.42 = (f32[80]{0:T(128)S(1)}, f32[80]{0:T(128)}, u32[]{:S(2)}) copy-start(f32[80]{0:T(128)} %copy-done.41) | copy-start | bytes 964
  346.7 256.1 %copy-start.17 = (bf16[80,5120]{1,0:T(8,128)(2,1)S(1)}, bf16[80,5120]{1,0:T(8,128)(2,1)}, u32[]{:S(2)}) copy-start(bf16[80,5120]{1,0:T(8,128)(2,1)} %param.45) | copy-start | bytes 2457604
  346.7 297.9 %reduce-scatter.5.cloned.1.call-start = ((), (), s32[]{:S(2)}) async-start(), calls=%async_computation.3 | async-start | bytes 2457600 | tf_op jit(solution)/shard_map/reduce_scatter | solution.py:143
  (40 other events, 131.8 us)
Sparse Core Ops, SparseCore 0:
  346.7 253.9 reduce-scatter.2
  603.0 26.4 reduce-scatter.4
where the time goes:
time: 666 us; the launch traced here: 654 us
  waiting for transfers between devices  254 us (38%)
  other arithmetic  105 us (16%)
  local copies, waits for them, and re-layouts  91.9 us (14%)
  matrix products  91.6 us (14%)
  loops' own time  55.7 us (8%)
  blocking collectives  40.1 us (6%)
  between operations  15.6 us (2%)
    reduce_scatter x1, waiting for transfers between devices, on_device(): lax.psum_scatter(fold_rows().astype(jnp.bfloat16), 'arc', scatter_dimensi...  254 us
    while x156, local copies, waits for them, and re-layouts  63.5 us
    another operation x1, loops' own time, fold_rows(): lax.map(one_block, jnp.arange(lax.axis_size('arc') * (half_width // membe...  55.5 us
    dot_general x38, matrix products, above_only(): lax.dot_general(above_cols, above_tile, contract_dims, preferred_element_...  46.1 us
    unnamed x1, blocking collectives  40.1 us
    dynamic_update_slice x4, other arithmetic, fold_rows(): lax.map(one_block, jnp.arange(lax.axis_size('arc') * (half_width // membe...  39.3 us
    another operation x4, other arithmetic, local_system(): jax.scipy.linalg.cho_solve((factor, True), coupling).astype(jnp.bfloat16)  32 us
    dot_general x18, matrix products, mirror_only(): lax.dot_general(mirror_cols, mirror_tile, contract_dims, preferred_elemen...  25.8 us
  transfers between devices with their start and end apart: 2, of which 1 were waited for; matrix products, arithmetic and copies ran while one was open for 0% of the time, Pallas kernels for 0%

commit v1 on v0

v1 whole, which is shorter than its diff:
```python
import functools

import jax
import jax.numpy as jnp
import numpy as np
from jax import lax
from jax.experimental import pallas as pl
from jax.experimental.pallas import tpu as pltpu
from jax.sharding import PartitionSpec as P

LANES = 128


def rounded_up(value, unit):
    return -(-value // unit) * unit


def projector_kernel(
    sizes_ref, kinds_ref, nuis_ref, arc_col_ref, arc_row_ref, kind_col_ref, obs_row_ref, out_ref
):
    rows, wide = out_ref.shape
    arc_col = arc_col_ref[...]
    kind_col = kind_col_ref[...]
    weight = jnp.zeros((rows, 1), jnp.float32)
    for kind in range(kinds_ref.shape[0]):
        weight = jnp.where(kind_col == kind, kinds_ref[kind], weight)
    size = jnp.zeros((rows, 1), jnp.int32)
    for arc in range(sizes_ref.shape[0]):
        size = jnp.where(arc_col == arc, sizes_ref[arc], size)
    nuis = nuis_ref[...].astype(jnp.float32)
    nuis = jnp.where(lax.broadcasted_iota(jnp.int32, nuis.shape, 1) < size, nuis, 0.0)
    padded = jnp.concatenate(
        [nuis, jnp.zeros((wide - rows, nuis.shape[1]), jnp.float32)], axis=0
    )
    gram = lax.dot_general(
        nuis.astype(jnp.bfloat16),
        padded.astype(jnp.bfloat16),
        (((1,), (1,)), ((), ())),
        preferred_element_type=jnp.float32,
    )
    lane = lax.broadcasted_iota(jnp.int32, (rows, wide), 1)
    sub = lax.broadcasted_iota(jnp.int32, (rows, wide), 0)
    state = jnp.where(arc_col == arc_row_ref[...], gram, 0.0)
    state = state + jnp.where(lane == sub, 1.0 / weight, 0.0)
    for k in range(rows):
        row = state[k : k + 1, :]
        col = state[:, k : k + 1]
        inv = 1.0 / row[:, k : k + 1]
        scaled_row = row * inv
        scaled_col = col * inv
        swept = state - col * scaled_row
        swept = jnp.where(lane == k, scaled_col, swept)
        swept = jnp.where(sub == k, scaled_row, swept)
        state = jnp.where((lane == k) & (sub == k), -inv, swept)
    inverse = -state
    reduced_obs = jnp.sum(inverse * obs_row_ref[...], axis=1, keepdims=True)
    out_ref[...] = jnp.where(lane == rows, reduced_obs, inverse).astype(out_ref.dtype)


def fold_kernel(
    block_rows,
    width,
    weight_ref,
    proj_ref,
    picked_ref,
    perm_ref,
    rows_ref,
    above_ref,
    mirror_ref,
    fold_ref,
    right_ref,
    tail_ref,
    lhs_ref,
):
    tile = pl.program_id(0)
    tile_cols = above_ref.shape[1]
    out_rows = fold_ref.shape[0]
    weight = weight_ref[0]

    @pl.when(tile == 0)
    def _():
        tail = jnp.zeros((1, width), jnp.float32)
        lane = lax.broadcasted_iota(jnp.int32, (block_rows, width), 1)
        pieces = []
        for block in range(proj_ref.shape[0] // block_rows):
            span = pl.ds(block * block_rows, block_rows)
            proj = proj_ref[span, :]
            picked = picked_ref[span, :]
            reduced = lax.dot_general(
                proj[:, :block_rows], picked, (((1,), (0,)), ((), ())),
                preferred_element_type=jnp.float32,
            )
            tail_reduced = reduced[:, 2 * width :].astype(jnp.bfloat16).astype(jnp.float32)
            tail += jnp.sum(
                picked[:, 2 * width :].astype(jnp.float32) * tail_reduced, axis=0, keepdims=True
            )
            first = jnp.where(
                lane == width - 1,
                proj[:, block_rows : block_rows + 1].astype(jnp.float32),
                reduced[:, :width],
            )
            second = jnp.dot(
                reduced[:, width : 2 * width].astype(jnp.bfloat16),
                perm_ref[...],
                preferred_element_type=jnp.float32,
            )
            pieces.append(jnp.concatenate([first, second], axis=1))
        lhs_ref[...] = jnp.concatenate(pieces, axis=0).T.astype(jnp.bfloat16)
        tail_ref[...] = weight * tail

    above = jnp.dot(
        lhs_ref[pl.ds(0, width), :], above_ref[...], preferred_element_type=jnp.float32
    )
    right_ref[...] = weight * above[width - 1 : width, :]
    mirror = jnp.dot(
        lhs_ref[pl.ds(width, rounded_up(out_rows, 16)), :],
        mirror_ref[...],
        preferred_element_type=jnp.float32,
    )[:out_rows]
    mirror = (weight * mirror).astype(jnp.bfloat16)
    flip = (
        lax.broadcasted_iota(jnp.int32, (LANES, LANES), 0)
        + lax.broadcasted_iota(jnp.int32, (LANES, LANES), 1)
        == LANES - 1
    ).astype(jnp.float32).astype(jnp.bfloat16)
    flipped = jnp.concatenate(
        [
            jnp.dot(
                mirror[:, start : start + LANES], flip, preferred_element_type=jnp.float32
            )
            for start in range(tile_cols - LANES, -1, -LANES)
        ],
        axis=1,
    )
    cols = lax.broadcasted_iota(jnp.int32, (out_rows, tile_cols), 1) + tile * tile_cols
    fold_ref[...] = jnp.where(
        cols >= rows_ref[...], weight * above[:out_rows], flipped
    ).astype(fold_ref.dtype)


def on_device(
    design,
    nuisance_design,
    observed,
    arc_of_row,
    nuis_size,
    weight_index,
    kind_weight,
    mission_weight,
):
    groups = lax.axis_size("mission")
    members = lax.axis_size("arc")
    group = lax.axis_index("mission")
    member = lax.axis_index("arc")
    block_rows, width_all = design.shape
    half_width = width_all // 2
    final_rows = half_width // (groups * members)
    out_rows = groups * final_rows
    wide = rounded_up(block_rows + 1, LANES)
    width = rounded_up(out_rows + 1, LANES)
    vmem = pl.BlockSpec(memory_space=pltpu.VMEM)
    smem = pl.BlockSpec(memory_space=pltpu.SMEM)

    design_all = lax.all_gather(design, "arc", axis=0, tiled=True)

    proj = pl.pallas_call(
        projector_kernel,
        out_shape=jax.ShapeDtypeStruct((block_rows, wide), jnp.bfloat16),
        in_specs=[smem, smem, vmem, vmem, vmem, vmem, vmem],
        out_specs=vmem,
        cost_estimate=pl.CostEstimate(flops=10_000_000, bytes_accessed=100_000, transcendentals=0),
        name="projector",
    )(
        nuis_size,
        kind_weight,
        nuisance_design,
        arc_of_row[:, None],
        jnp.pad(arc_of_row, (0, wide - block_rows), constant_values=-1)[None, :],
        weight_index[:, None],
        jnp.pad(observed, (0, wide - block_rows))[None, :],
    )
    proj_all = lax.all_gather(proj, "arc", axis=0, tiled=True)

    def picked(start_of):
        parts = [
            lax.dynamic_slice_in_dim(
                design_all, start_of(other * members + member), final_rows, 1
            )
            for other in range(groups)
        ]
        blank = jnp.zeros((design_all.shape[0], width - out_rows), design_all.dtype)
        return parts + [blank]

    picked_all = jnp.concatenate(
        picked(lambda block: block * final_rows)
        + picked(lambda block: width_all - (block + 1) * final_rows)
        + picked(lambda block: half_width + block * final_rows),
        axis=1,
    )
    place = np.arange(out_rows)
    perm = np.zeros((width, width), np.float32)
    perm[(place // final_rows) * final_rows + final_rows - 1 - place % final_rows, place] = 1.0
    row_ids = (
        (jnp.arange(groups, dtype=jnp.int32)[:, None] * members + member) * final_rows
        + jnp.arange(final_rows, dtype=jnp.int32)[None, :]
    ).reshape(out_rows, 1)

    tile_cols = 512
    tiles = width_all // tile_cols
    all_rows = design_all.shape[0]
    whole = lambda shape: pl.BlockSpec(shape, lambda j: (0, 0))
    fold, right, tail = pl.pallas_call(
        functools.partial(fold_kernel, block_rows, width),
        grid=(tiles,),
        out_shape=(
            jax.ShapeDtypeStruct((out_rows, width_all), jnp.bfloat16),
            jax.ShapeDtypeStruct((1, width_all), jnp.float32),
            jax.ShapeDtypeStruct((1, width), jnp.float32),
        ),
        in_specs=[
            smem,
            whole((all_rows, wide)),
            whole((all_rows, 3 * width)),
            whole((width, width)),
            whole((out_rows, 1)),
            pl.BlockSpec((all_rows, tile_cols), lambda j: (0, j)),
            pl.BlockSpec((all_rows, tile_cols), lambda j: (0, tiles - 1 - j)),
        ],
        out_specs=(
            pl.BlockSpec((out_rows, tile_cols), lambda j: (0, j)),
            pl.BlockSpec((1, tile_cols), lambda j: (0, j)),
            whole((1, width)),
        ),
        scratch_shapes=[pltpu.VMEM((2 * width, all_rows), jnp.bfloat16)],
        compiler_params=pltpu.CompilerParams(
            dimension_semantics=("arbitrary",), vmem_limit_bytes=60 * 2**20
        ),
        cost_estimate=pl.CostEstimate(
            flops=4 * width * all_rows * width_all,
            bytes_accessed=4 * all_rows * width_all,
            transcendentals=0,
        ),
        name="fold",
    )(
        mission_weight,
        proj_all,
        picked_all,
        jnp.asarray(perm, jnp.bfloat16),
        row_ids,
        design_all,
        design_all,
    )

    right_own = lax.dynamic_index_in_dim(
        right.reshape(groups, members, width_all // (groups * members)), member, 1, keepdims=False
    )
    tail_own = tail[0, :out_rows].reshape(groups, final_rows)
    fold = fold.reshape(groups, final_rows, width_all)
    vectors = jnp.concatenate([right_own, tail_own], axis=1)

    def taken(array, index):
        return lax.dynamic_index_in_dim(array, index, 0, keepdims=False)

    fold_total = taken(fold, group).astype(jnp.float32)
    vector_total = taken(vectors, group)
    for shift in range(1, groups):
        ring = [(source, (source + shift) % groups) for source in range(groups)]
        target = (group + shift) % groups
        fold_total += lax.ppermute(taken(fold, target), "mission", ring).astype(jnp.float32)
        vector_total += lax.ppermute(taken(vectors, target), "mission", ring)
    split = right_own.shape[1]
    return (fold_total, vector_total[:split], vector_total[split:])


def solution(mesh):
    placed = (
        P(("mission", "arc"), None),
        P(("mission", "arc"), None),
        P(("mission", "arc")),
        P(("mission", "arc")),
        P(("mission", "arc")),
        P(("mission", "arc")),
        P(),
        P("mission"),
    )
    return jax.shard_map(
        on_device,
        mesh=mesh,
        in_specs=placed,
        out_specs=(P(("mission", "arc"), None), P(("mission", "arc")), P(("mission", "arc"))),
        check_vma=False,
    )
```

time: 666 us -> 174 us (0.26); the launches traced: 654 us -> 173 us
  waiting for transfers between devices: 254 us -> 80.6 us
  other arithmetic: 105 us -> 2.94 us
  matrix products: 91.6 us -> 0 us
  local copies, waits for them, and re-layouts: 91.9 us -> 14.3 us
  loops' own time: 55.7 us -> 0 us
  Pallas kernels: 0 us -> 30.4 us
  blocking collectives: 40.1 us -> 28 us
    reduce_scatter x2 -> x0, waiting for transfers between devices: 254 us -> none  [the longest x1 254 us: on_device(): lax.psum_scatter(fold_rows().astype(jnp.bfloat16), 'arc', scatter_dimensi...]
    dot_general x65 -> x0, matrix products: 79.6 us -> none  [the longest x38 46.1 us: above_only(): lax.dot_general(above_cols, above_tile, contract_dims, preferred_element_...]
    all_gather x0 -> x1, waiting for transfers between devices: none -> 63.7 us  [on_device(): design_all = lax.all_gather(design, 'arc', axis=0, tiled=True)]
    while x156 -> x0, local copies, waits for them, and re-layouts: 63.5 us -> none
    another operation x10 -> x0, other arithmetic: 56.8 us -> none  [the longest x4 32 us: local_system(): jax.scipy.linalg.cho_solve((factor, True), coupling).astype(jnp.bfloat16)]
    another operation x41 -> x0, loops' own time: 55.7 us -> none  [the longest x1 55.5 us: fold_rows(): lax.map(one_block, jnp.arange(lax.axis_size('arc') * (half_width // membe...]
    unnamed x1 -> x0, blocking collectives: 40.1 us -> none
    dynamic_update_slice x4 -> x0, other arithmetic: 39.3 us -> none  [fold_rows(): lax.map(one_block, jnp.arange(lax.axis_size('arc') * (half_width // membe...]
  transfers between devices with their start and end apart: 2 -> 3, of which waited for: 1 -> 2; matrix products, arithmetic and copies ran while one was open for 0% -> 5% of each run, Pallas kernels for 0% -> 7%
where the time goes in v1:
time: 174 us; the launch traced here: 173 us
  waiting for transfers between devices  80.6 us (46%)
  Pallas kernels  30.4 us (17%)
  blocking collectives  28 us (16%)
  between operations  14.8 us (9%)
  local copies, waits for them, and re-layouts  14.3 us (8%)
  other arithmetic  2.94 us (2%)
  starting transfers between devices  2.13 us (1%)
    all_gather x1, waiting for transfers between devices, on_device(): design_all = lax.all_gather(design, 'arc', axis=0, tiled=True)  63.7 us
    all_gather x1, blocking collectives, on_device(): proj_all = lax.all_gather(proj, 'arc', axis=0, tiled=True)  28 us
    pallas_call x1, Pallas kernels, on_device(): pl.pallas_call(functools.partial(fold_kernel, block_rows, width), grid=(t...  18.1 us
    ppermute x1, waiting for transfers between devices, on_device(): vector_total += lax.ppermute(taken(vectors, target), 'mission', ring)  16.3 us
    pallas_call x1, Pallas kernels, on_device(): pl.pallas_call(projector_kernel, out_shape=jax.ShapeDtypeStruct((block_ro...  12.3 us
  transfers between devices with their start and end apart: 3, of which 2 were waited for; matrix products, arithmetic and copies ran while one was open for 5% of the time, Pallas kernels for 7%

profile of v1, /device:TPU:0, one launch (start us, length us, event | category | flops | bytes accessed | tf_op | source)
XLA Modules:
  0.0 173.2 jit_solution(3927147812028559637)
XLA Ops:
  7.2 0.0 all-gather.2.cloned.1.call-start
  7.2 0.7 all-gather.2.cloned.1.call-update
  7.9 0.1 iota_add_fusion
  8.0 0.8 add.129.rows_ref
  8.8 1.4 copy.14.arc_col_ref
  10.2 1.4 copy.15.kind_col_ref
  12.2 1.2 pad_bitcast_fusion.1.arc_row_ref
  13.3 1.2 pad_bitcast_fusion.obs_row_ref
  14.5 12.3 %projector.1 = bf16[80,128]{1,0:T(8,128)(2,1)} custom-call(s32[2]{0:T(128)} %sizes_ref.1, f32[8]{0:T(128)} %kinds_ref.1, bf16[80,128]{1,0:T(8,128)(2,1)} %nuis_ref.1, s32[80,1]{1,0:T(8,128)} %copy.14.arc_col_ref, s32[1,128]{1,0:T(1,128)} %pad_bitcast_fusion.1.arc_row_ref, s32[80,1]{1,0:T(8,128)} %copy.15.kind_col_ref, f32[1,128]{1,0:T(1,128)} %pad_bitcast_fusion.obs_row_ref), custom_call_target="tpu_custom_call" | custom-call | flops 10000000 | bytes 100000 | tf_op jit(solution)/shard_map/projector/pallas_call | solution.py:166
  26.8 28.0 %all_gather.6.proj_ref = bf16[1280,128]{1,0:T(8,128)(2,1)} all-gather(bf16[80,128]{1,0:T(8,128)(2,1)} %projector.1), channel_id=1, replica_groups=mesh['mission'=2,'arc'=16] {'arc'}, dimensions={0}, use_global_device_ids=true | all-gather | bytes 348160 | tf_op jit(solution)/shard_map/all_gather | solution.py:182
  54.8 63.7 %all-gather.2.cloned.1.call-done.above_ref.mirror_ref = bf16[1280,5120]{1,0:T(8,128)(2,1)} async-done(((bf16[80,5120]{1,0:T(8,128)(2,1)}), bf16[1280,5120]{1,0:T(8,128)(2,1)}) %all-gather.2.cloned.1.call-update) | async-done | bytes 13107216 | tf_op jit(solution)/shard_map/all_gather | solution.py:164
  118.5 2.7 %constant_dynamic-slice_fusion.5 = (bf16[1280,80]{1,0:T(8,128)(2,1)S(1)}, bf16[1280,80]{1,0:T(8,128)(2,1)S(1)}, bf16[1280,80]{1,0:T(8,128)(2,1)S(1)}, bf16[1280,...) fusion(bf16[1280,5120]{1,0:T(8,128)(2,1)} %all-gather.2.cloned.1.call-done.above_ref.mirror_ref, ...), kind=kLoop, calls=%fused_computation.7 | loop fusion | bytes 2457624 | tf_op jit(solution)/shard_map/dynamic_slice | solution.py:186
  121.3 3.1 %concatenate.6.picked_ref = bf16[1280,768]{1,0:T(8,128)(2,1)} concatenate(bf16[1280,80]{1,0:T(8,128)(2,1)S(1)} %get-tuple-element.14, bf16[1280,80]{1,0:T(8,128)(2,1)S(1)} %get-tuple-element.13, bf16[1280,96]{1,0:T(8,128)(2,1)S(1)} %broadcast.33, bf16[1280,80]{1,0:T(8,128)(2,1)S(1)} %get-tuple-element.12, bf16[1280,80]{1,0:T(8,128)(2,1)S(1)} %get-tuple-element.11, ...), dimensions={1} | concatenate | bytes 3932160 | tf_op jit(solution)/shard_map/concatenate | solution.py:194
  124.3 18.1 %fold.1 = (bf16[160,5120]{1,0:T(8,128)(2,1)}, f32[1,5120]{1,0:T(1,128)}, f32[1,256]{1,0:T(1,128)}) custom-call(f32[1]{0:T(128)S(6)} %copy.20.weight_ref, bf16[1280,128]{1,0:T(8,128)(2,1)} %all_gather.6.proj_ref, bf16[1280,768]{1,0:T(8,128)(2,1)} %concatenate.6.picked_ref, bf16[256,256]{1,0:T(8,128)(2,1)} %constant.66.clone.perm_ref, ...), custom_call_target="tpu_custom_call" | custom-call | flops 6710886400 | bytes 26214400 | tf_op jit(solution)/shard_map/fold/pallas_call | solution.py:212
  142.4 0.0 copy-start.2
  142.4 0.0 copy-start
  142.4 1.3 dynamic-slice_bitcast_fusion
  143.8 1.5 collective-permute-start
  145.3 0.5 broadcast.44
  145.8 1.4 reduce.7
  147.2 0.1 reshape.47
  147.3 0.0 copy-done.2
  147.4 0.1 reshape_squeeze.3
  147.4 0.1 fusion.1
  147.5 0.6 collective-permute-start.1
  148.1 16.3 %collective-permute-done.1 = f32[240]{0:T(256)S(1)} collective-permute-done((f32[240]{0:T(256)S(1)}, f32[240]{0:T(256)S(1)}, u32[]{:S(2)}, u32[]{:S(2)}) %collective-permute-start.1) | collective-permute-done | bytes 992 | tf_op jit(solution)/shard_map/ppermute | solution.py:270
  164.4 0.0 copy-start.1
  164.4 0.6 slice.11
  165.0 0.0 collective-permute-done
  165.0 0.0 copy-done
  165.0 1.4 convert_add_fusion
  166.3 0.0 copy-done.1
  (6 shorter events, 0.1 us)
Async XLA Ops:
  7.2 111.3 %all-gather.2.cloned.1.call-start = ((), (), s32[]{:S(2)}) async-start(), calls=%async_computation | async-start | bytes 13926400 | tf_op jit(solution)/shard_map/all_gather | solution.py:164
  142.4 4.9 %copy-start.2 = (f32[1,256]{1,0:T(1,128)S(1)}, f32[1,256]{1,0:T(1,128)}, u32[]{:S(2)}) copy-start(f32[1,256]{1,0:T(1,128)} %get-tuple-element.8) | copy-start | bytes 3076
  142.4 22.6 %copy-start = (bf16[160,5120]{1,0:T(8,128)(2,1)S(1)}, bf16[160,5120]{1,0:T(8,128)(2,1)}, u32[]{:S(2)}) copy-start(bf16[160,5120]{1,0:T(8,128)(2,1)} %get-tuple-element.6) | copy-start | bytes 4915204
  143.8 21.2 %collective-permute-start = (bf16[80,5120]{1,0:T(8,128)(2,1)S(1)}, bf16[80,5120]{1,0:T(8,128)(2,1)S(1)}, u32[]{:S(2)}, u32[]{:S(2)}) collective-permute-start(bf16[80,5120]{1,0:T(8,128)(2,1)S(1)} %dynamic-slice_bitcast_fusion), channel_id=1, source_target_pairs={{0,16},{16,0},{1,17},{17,1},{2,18},{18,2},{3,19},{19,3},{4,20},{20... | collective-permute-start | bytes 2457608 | tf_op jit(solution)/shard_map/ppermute | solution.py:269
  147.5 16.9 %collective-permute-start.1 = (f32[240]{0:T(256)S(1)}, f32[240]{0:T(256)S(1)}, u32[]{:S(2)}, u32[]{:S(2)}) collective-permute-start(f32[240]{0:T(256)S(1)} %bitcast.23), channel_id=1, source_target_pairs={{0,16},{16,0},{1,17},{17,1},{2,18},{18,2},{3,19},{19,3},{4,20},{20... | collective-permute-start | bytes 2888 | tf_op jit(solution)/shard_map/ppermute | solution.py:270
  164.4 1.9 %copy-start.1 = (f32[240]{0:T(256)}, f32[240]{0:T(256)S(1)}, u32[]{:S(2)}) copy-start(f32[240]{0:T(256)S(1)} %add.128) | copy-start | bytes 2884
Sparse Core Ops, SparseCore 0:
  10.3 108.1 all-gather.1

commit v2 on v1

v2 whole, which is shorter than its diff:
```python
import functools

import jax
import jax.numpy as jnp
import numpy as np
from jax import lax
from jax.experimental import pallas as pl
from jax.experimental.pallas import tpu as pltpu
from jax.sharding import PartitionSpec as P

LANES = 128


def rounded_up(value, unit):
    return -(-value // unit) * unit


def projector_kernel(
    sizes_ref, kinds_ref, nuis_ref, arc_col_ref, arc_row_ref, kind_col_ref, obs_row_ref, out_ref
):
    rows, wide = out_ref.shape
    arc_col = arc_col_ref[...]
    kind_col = kind_col_ref[...]
    weight = jnp.zeros((rows, 1), jnp.float32)
    for kind in range(kinds_ref.shape[0]):
        weight = jnp.where(kind_col == kind, kinds_ref[kind], weight)
    size = jnp.zeros((rows, 1), jnp.int32)
    for arc in range(sizes_ref.shape[0]):
        size = jnp.where(arc_col == arc, sizes_ref[arc], size)
    nuis = nuis_ref[...].astype(jnp.float32)
    nuis = jnp.where(lax.broadcasted_iota(jnp.int32, nuis.shape, 1) < size, nuis, 0.0)
    padded = jnp.concatenate(
        [nuis, jnp.zeros((wide - rows, nuis.shape[1]), jnp.float32)], axis=0
    )
    gram = lax.dot_general(
        nuis.astype(jnp.bfloat16),
        padded.astype(jnp.bfloat16),
        (((1,), (1,)), ((), ())),
        preferred_element_type=jnp.float32,
    )
    lane = lax.broadcasted_iota(jnp.int32, (rows, wide), 1)
    sub = lax.broadcasted_iota(jnp.int32, (rows, wide), 0)
    state = jnp.where(arc_col == arc_row_ref[...], gram, 0.0)
    state = state + jnp.where(lane == sub, 1.0 / weight, 0.0)
    for k in range(rows):
        row = state[k : k + 1, :]
        col = state[:, k : k + 1]
        inv = 1.0 / row[:, k : k + 1]
        scaled_row = row * inv
        scaled_col = col * inv
        swept = state - col * scaled_row
        swept = jnp.where(lane == k, scaled_col, swept)
        swept = jnp.where(sub == k, scaled_row, swept)
        state = jnp.where((lane == k) & (sub == k), -inv, swept)
    inverse = -state
    reduced_obs = jnp.sum(inverse * obs_row_ref[...], axis=1, keepdims=True)
    out_ref[...] = jnp.where(lane == rows, reduced_obs, inverse).astype(out_ref.dtype)


def fold_kernel(
    block_rows,
    width,
    with_right,
    weight_ref,
    span_ref,
    proj_ref,
    picked_ref,
    perm_ref,
    rows_ref,
    above_ref,
    mirror_ref,
    fold_ref,
    tail_ref,
    *rest,
):
    lhs_ref = rest[-1]
    tile = pl.program_id(0)
    tile_cols = above_ref.shape[1]
    out_rows = fold_ref.shape[0]
    weight = weight_ref[0]

    @pl.when(tile == 0)
    def _():
        tail = jnp.zeros((1, width), jnp.float32)
        lane = lax.broadcasted_iota(jnp.int32, (block_rows, width), 1)
        pieces = []
        for block in range(proj_ref.shape[0] // block_rows):
            span = pl.ds(block * block_rows, block_rows)
            proj = proj_ref[span, :]
            picked = picked_ref[span, :]
            reduced = lax.dot_general(
                proj[:, :block_rows], picked, (((1,), (0,)), ((), ())),
                preferred_element_type=jnp.float32,
            )
            tail_reduced = reduced[:, 2 * width :].astype(jnp.bfloat16).astype(jnp.float32)
            tail += jnp.sum(
                picked[:, 2 * width :].astype(jnp.float32) * tail_reduced, axis=0, keepdims=True
            )
            first = jnp.where(
                lane == width - 1,
                proj[:, block_rows : block_rows + 1].astype(jnp.float32),
                reduced[:, :width],
            )
            second = jnp.dot(
                reduced[:, width : 2 * width].astype(jnp.bfloat16),
                perm_ref[...],
                preferred_element_type=jnp.float32,
            )
            pieces.append(jnp.concatenate([first, second], axis=1))
        lhs_ref[...] = jnp.concatenate(pieces, axis=0).T.astype(jnp.bfloat16)
        tail_ref[...] = weight * tail

    low, high = span_ref[0], span_ref[1]
    col_start = tile * tile_cols
    all_above = col_start >= high
    all_mirror = col_start + tile_cols <= low

    def above_tile():
        return weight * jnp.dot(
            lhs_ref[pl.ds(0, width), :], above_ref[...], preferred_element_type=jnp.float32
        )

    def mirror_tile():
        mirror = jnp.dot(
            lhs_ref[pl.ds(width, rounded_up(out_rows, 16)), :],
            mirror_ref[...],
            preferred_element_type=jnp.float32,
        )[:out_rows]
        mirror = (weight * mirror).astype(jnp.bfloat16)
        flip = (
            lax.broadcasted_iota(jnp.int32, (LANES, LANES), 0)
            + lax.broadcasted_iota(jnp.int32, (LANES, LANES), 1)
            == LANES - 1
        ).astype(jnp.float32).astype(jnp.bfloat16)
        return jnp.concatenate(
            [
                jnp.dot(
                    mirror[:, start : start + LANES], flip, preferred_element_type=jnp.float32
                )
                for start in range(tile_cols - LANES, -1, -LANES)
            ],
            axis=1,
        )

    if with_right:
        above = above_tile()
        rest[0][...] = above[width - 1 : width, :]
        fold_ref[...] = above[:out_rows].astype(fold_ref.dtype)
    else:

        @pl.when(jnp.logical_not(all_mirror))
        def _():
            fold_ref[...] = above_tile()[:out_rows].astype(fold_ref.dtype)

    @pl.when(all_mirror)
    def _():
        fold_ref[...] = mirror_tile().astype(fold_ref.dtype)

    @pl.when(jnp.logical_not(jnp.logical_or(all_above, all_mirror)))
    def _():
        cols = lax.broadcasted_iota(jnp.int32, (out_rows, tile_cols), 1) + col_start
        fold_ref[...] = jnp.where(
            cols >= rows_ref[...], fold_ref[...].astype(jnp.float32), mirror_tile()
        ).astype(fold_ref.dtype)


def on_device(
    design,
    nuisance_design,
    observed,
    arc_of_row,
    nuis_size,
    weight_index,
    kind_weight,
    mission_weight,
):
    groups = lax.axis_size("mission")
    members = lax.axis_size("arc")
    group = lax.axis_index("mission")
    member = lax.axis_index("arc")
    block_rows, width_all = design.shape
    half_width = width_all // 2
    final_rows = half_width // (groups * members)
    wide = rounded_up(block_rows + 1, LANES)
    inner = 2 if members % 2 == 0 else 1
    outer = 4 if members % (4 * inner) == 0 else 1
    mid = members // (outer * inner)
    mid_at = (member // inner) % mid
    gather_groups = [
        [(o * mid + y) * inner + c for o in range(outer) for c in range(inner)]
        for y in range(mid)
    ]

    def gathered(array):
        return lax.all_gather(
            array, "arc", axis=0, tiled=True, axis_index_groups=gather_groups
        )

    def member_of(y):
        return (member // (inner * mid) * mid + y) * inner + member % inner

    vmem = pl.BlockSpec(memory_space=pltpu.VMEM)
    smem = pl.BlockSpec(memory_space=pltpu.SMEM)

    design_all = gathered(design)

    proj = pl.pallas_call(
        projector_kernel,
        out_shape=jax.ShapeDtypeStruct((block_rows, wide), jnp.bfloat16),
        in_specs=[smem, smem, vmem, vmem, vmem, vmem, vmem],
        out_specs=vmem,
        cost_estimate=pl.CostEstimate(flops=10_000_000, bytes_accessed=100_000, transcendentals=0),
        name="projector",
    )(
        nuis_size,
        kind_weight,
        nuisance_design,
        arc_of_row[:, None],
        jnp.pad(arc_of_row, (0, wide - block_rows), constant_values=-1)[None, :],
        weight_index[:, None],
        jnp.pad(observed, (0, wide - block_rows))[None, :],
    )
    proj_all = gathered(proj)

    shifts = [(dm, dy) for dm in range(groups) for dy in range(mid)]
    shifts.sort(key=lambda shift: -(shift[0] > 0) - (shift[1] > 0))
    per_call = max(1, len(shifts) // 4)
    out_rows = per_call * final_rows
    width = rounded_up(out_rows + 1, LANES)
    place = np.arange(out_rows)
    perm = np.zeros((width, width), np.float32)
    perm[(place // final_rows) * final_rows + final_rows - 1 - place % final_rows, place] = 1.0
    tile_cols = 512
    tiles = width_all // tile_cols
    all_rows = design_all.shape[0]
    right_cols = width_all // (groups * members)
    whole = lambda shape: pl.BlockSpec(shape, lambda j: (0, 0))

    def fold_call(owners, with_right):
        def picked(start_of):
            parts = [
                lax.dynamic_slice_in_dim(design_all, start_of(owner), final_rows, 1)
                for owner in owners
            ]
            blank = jnp.zeros((all_rows, width - out_rows), design_all.dtype)
            return parts + [blank]

        picked_all = jnp.concatenate(
            picked(lambda block: block * final_rows)
            + picked(lambda block: width_all - (block + 1) * final_rows)
            + picked(lambda block: half_width + block * final_rows),
            axis=1,
        )
        starts = jnp.stack(owners).astype(jnp.int32) * final_rows
        row_ids = (
            starts[:, None] + jnp.arange(final_rows, dtype=jnp.int32)[None, :]
        ).reshape(out_rows, 1)
        span = jnp.stack([jnp.min(starts), jnp.max(starts) + final_rows - 1])
        out_shape = [
            jax.ShapeDtypeStruct((out_rows, width_all), jnp.bfloat16),
            jax.ShapeDtypeStruct((1, width), jnp.float32),
        ]
        out_specs = [
            pl.BlockSpec((out_rows, tile_cols), lambda j: (0, j)),
            whole((1, width)),
        ]
        if with_right:
            out_shape.append(jax.ShapeDtypeStruct((1, width_all), jnp.float32))
            out_specs.append(pl.BlockSpec((1, tile_cols), lambda j: (0, j)))
        return pl.pallas_call(
            functools.partial(fold_kernel, block_rows, width, with_right),
            grid=(tiles,),
            out_shape=tuple(out_shape),
            in_specs=[
                smem,
                smem,
                whole((all_rows, wide)),
                whole((all_rows, 3 * width)),
                whole((width, width)),
                whole((out_rows, 1)),
                pl.BlockSpec((all_rows, tile_cols), lambda j: (0, j)),
                pl.BlockSpec((all_rows, tile_cols), lambda j: (0, tiles - 1 - j)),
            ],
            out_specs=tuple(out_specs),
            scratch_shapes=[pltpu.VMEM((2 * width, all_rows), jnp.bfloat16)],
            compiler_params=pltpu.CompilerParams(
                dimension_semantics=("arbitrary",), vmem_limit_bytes=60 * 2**20
            ),
            cost_estimate=pl.CostEstimate(
                flops=4 * width * all_rows * width_all,
                bytes_accessed=4 * all_rows * width_all,
                transcendentals=0,
            ),
            name="fold",
        )(
            mission_weight,
            span,
            proj_all,
            picked_all,
            jnp.asarray(perm, jnp.bfloat16),
            row_ids,
            design_all,
            design_all,
        )

    def ring(dm, dy):
        pairs = []
        for m in range(groups):
            for a in range(members):
                o, y, c = a // (inner * mid), (a // inner) % mid, a % inner
                target = (o * mid + (y + dy) % mid) * inner + c
                pairs.append((m * members + a, (m + dm) % groups * members + target))
        return pairs

    right = None
    folds, vectors = [], []
    for first in range(0, len(shifts), per_call):
        here = shifts[first : first + per_call]
        owners = [
            (group + dm) % groups * members + member_of((mid_at + dy) % mid) for dm, dy in here
        ]
        fold, tail, *extra = fold_call(owners, right is None)
        if right is None:
            right = extra[0][0]
        for at, (dm, dy) in enumerate(here):
            rows = slice(at * final_rows, (at + 1) * final_rows)
            block = fold[rows]
            vector = jnp.concatenate(
                [
                    lax.dynamic_slice_in_dim(right, owners[at] * right_cols, right_cols),
                    tail[0, rows],
                ]
            )
            if dm or dy:
                block = lax.ppermute(block, ("mission", "arc"), ring(dm, dy))
                vector = lax.ppermute(vector, ("mission", "arc"), ring(dm, dy))
            folds.append(block.astype(jnp.float32))
            vectors.append(vector)
    fold_total = functools.reduce(jnp.add, folds)
    vector_total = functools.reduce(jnp.add, vectors)
    return (fold_total, vector_total[:right_cols], vector_total[right_cols:])


def solution(mesh):
    placed = (
        P(("mission", "arc"), None),
        P(("mission", "arc"), None),
        P(("mission", "arc")),
        P(("mission", "arc")),
        P(("mission", "arc")),
        P(("mission", "arc")),
        P(),
        P("mission"),
    )
    return jax.shard_map(
        on_device,
        mesh=mesh,
        in_specs=placed,
        out_specs=(P(("mission", "arc"), None), P(("mission", "arc")), P(("mission", "arc"))),
        check_vma=False,
    )
```

time: 174 us -> 163 us (0.937)
  waiting for transfers between devices: 80.6 us -> 42.4 us
  Pallas kernels: 30.4 us -> 57.4 us
  blocking collectives: 28 us -> 17.7 us
  starting transfers between devices: 2.13 us -> 7.05 us
  other arithmetic: 2.94 us -> 6.77 us
    all_gather x1, waiting for transfers between devices: 63.7 us -> 32.8 us  [gathered(): lax.all_gather(array, 'arc', axis=0, tiled=True, axis_index_groups=gather...]
    pallas_call x1 -> x4, Pallas kernels: 18.1 us -> 45.1 us  [fold_call(): pl.pallas_call(functools.partial(fold_kernel, block_rows, width, with_rig...]
    all_gather x1, blocking collectives: 28 us -> 17.7 us  [gathered(): lax.all_gather(array, 'arc', axis=0, tiled=True, axis_index_groups=gather...]
    ppermute x2 -> x6, waiting for transfers between devices: 16.3 us -> 8.97 us  [the longest x3 8.96 us: on_device(): vector = lax.ppermute(vector, ('mission', 'arc'), ring(dm, dy))]
    ppermute x2 -> x6, starting transfers between devices: 2.09 us -> 7.01 us  [the longest x3 3.56 us: on_device(): vector = lax.ppermute(vector, ('mission', 'arc'), ring(dm, dy))]
    add x3 -> x6, other arithmetic: 1.43 us -> 5.24 us  [the longest x1 2.69 us: on_device(): fold_total = functools.reduce(jnp.add, folds)]
    concatenate x1 -> x4, local copies, waits for them, and re-layouts: 3.08 us -> 4.45 us  [fold_call(): jnp.concatenate(picked(lambda block: block * final_rows) + picked(lambda...]
  transfers between devices with their start and end apart: 3 -> 7, of which waited for: 2 -> 2; matrix products, arithmetic and copies ran while one was open for 5% -> 8% of each run, Pallas kernels for 7% -> 21%
where the time goes in v2:
time: 163 us; the launch traced here: 162 us
  Pallas kernels  57.4 us (35%)
  waiting for transfers between devices  42.4 us (26%)
  blocking collectives  17.7 us (11%)
  local copies, waits for them, and re-layouts  15.8 us (10%)
  between operations  15 us (9%)
  starting transfers between devices  7.05 us (4%)
  other arithmetic  6.77 us (4%)
    pallas_call x4, Pallas kernels, fold_call(): pl.pallas_call(functools.partial(fold_kernel, block_rows, width, with_rig...  45.1 us
    all_gather x1, waiting for transfers between devices, gathered(): lax.all_gather(array, 'arc', axis=0, tiled=True, axis_index_groups=gather...  32.8 us
    all_gather x1, blocking collectives, gathered(): lax.all_gather(array, 'arc', axis=0, tiled=True, axis_index_groups=gather...  17.7 us
    pallas_call x1, Pallas kernels, on_device(): pl.pallas_call(projector_kernel, out_shape=jax.ShapeDtypeStruct((block_ro...  12.3 us
    ppermute x3, waiting for transfers between devices, on_device(): vector = lax.ppermute(vector, ('mission', 'arc'), ring(dm, dy))  8.96 us
    concatenate x4, local copies, waits for them, and re-layouts, fold_call(): jnp.concatenate(picked(lambda block: block * final_rows) + picked(lambda...  4.45 us
    ppermute x3, starting transfers between devices, on_device(): vector = lax.ppermute(vector, ('mission', 'arc'), ring(dm, dy))  3.56 us
    ppermute x3, starting transfers between devices, on_device(): block = lax.ppermute(block, ('mission', 'arc'), ring(dm, dy))  3.46 us
  transfers between devices with their start and end apart: 7, of which 2 were waited for; matrix products, arithmetic and copies ran while one was open for 8% of the time, Pallas kernels for 21%

profile of v2, /device:TPU:0, one launch (start us, length us, event | category | flops | bytes accessed | tf_op | source)
XLA Modules:
  0.0 162.1 jit_solution(9528127738356611958)
XLA Ops:
  7.2 0.0 all-gather.2.cloned.1.call-start
  7.2 0.7 all-gather.2.cloned.1.call-update
  8.1 1.4 copy.15.arc_col_ref
  9.4 1.4 copy.16.kind_col_ref
  11.6 1.2 pad_bitcast_fusion.1.arc_row_ref
  12.8 1.2 pad_bitcast_fusion.obs_row_ref
  13.9 12.3 %projector.1 = bf16[80,128]{1,0:T(8,128)(2,1)} custom-call(s32[2]{0:T(128)} %sizes_ref.1, f32[8]{0:T(128)} %kinds_ref.1, bf16[80,128]{1,0:T(8,128)(2,1)} %nuis_ref.1, s32[80,1]{1,0:T(8,128)} %copy.15.arc_col_ref, s32[1,128]{1,0:T(1,128)} %pad_bitcast_fusion.1.arc_row_ref, s32[80,1]{1,0:T(8,128)} %copy.16.kind_col_ref, f32[1,128]{1,0:T(1,128)} %pad_bitcast_fusion.obs_row_ref), custom_call_target="tpu_custom_call" | custom-call | flops 10000000 | bytes 100000 | tf_op jit(solution)/shard_map/projector/pallas_call | solution.py:207
  26.3 17.7 %all_gather.6.proj_ref = bf16[640,128]{1,0:T(8,128)(2,1)} all-gather(bf16[80,128]{1,0:T(8,128)(2,1)} %projector.1), channel_id=1, replica_groups={{0,1,4,5,8,9,12,13},{2,3,6,7,10,11,14,15},{16,17,20,21,24,25,28,29},{18..., dimensions={0}, use_global_device_ids=true | all-gather | bytes 184320 | tf_op jit(solution)/shard_map/all_gather | solution.py:195
  44.0 0.6 pad_add_fusion
  44.6 0.7 pad_add_fusion.2
  45.3 0.6 iota_add_fusion.3.rows_ref
  45.9 0.6 iota_add_fusion.2.rows_ref
  46.5 0.6 iota_add_fusion.1.rows_ref
  47.1 0.6 iota_add_fusion.rows_ref
  47.8 32.8 %all-gather.2.cloned.1.call-done.above_ref.mirror_ref = bf16[640,5120]{1,0:T(8,128)(2,1)} async-done(((bf16[80,5120]{1,0:T(8,128)(2,1)}), bf16[640,5120]{1,0:T(8,128)(2,1)}) %all-gather.2.cloned.1.call-update) | async-done | bytes 6553616 | tf_op jit(solution)/shard_map/all_gather | solution.py:195
  80.6 2.8 %constant_dynamic-slice_fusion.13 = (bf16[640,80]{1,0:T(8,128)(2,1)S(1)}, bf16[640,80]{1,0:T(8,128)(2,1)S(1)}, bf16[640,80]{1,0:T(8,128)(2,1)S(1)}, bf16[640,80]...) fusion(bf16[640,5120]{1,0:T(8,128)(2,1)} %all-gather.2.cloned.1, ...), kind=kLoop, calls=%fused_computation.18 | loop fusion | bytes 2457648 | tf_op jit(solution)/shard_map/dynamic_slice | solution.py:242
  83.4 1.1 concatenate.25.picked_ref
  84.5 11.2 %fold.5 = (bf16[80,5120]{1,0:T(8,128)(2,1)}, f32[1,128]{1,0:T(1,128)}) custom-call(f32[1]{0:T(128)S(6)} %copy.17.weight_ref, s32[2]{0:T(128)} %get-tuple-element.38.span_ref, bf16[640,128]{1,0:T(8,128)(2,1)} %all_gather.6.proj_ref, bf16[640,384]{1,0:T(8,128)(2,1)} %concatenate.25.picked_ref, bf16[128,128]{1,0:T(8,128)(2,1)} %constant.132.clone.perm_ref, ...), custom_call_target="tpu_custom_call" | custom-call | flops 1677721600 | bytes 13107200 | tf_op jit(solution)/shard_map/fold/pallas_call | solution.py:270
  95.7 0.7 slice_bitcast_fusion.2
  96.3 1.1 concatenate.24.picked_ref
  97.4 11.5 %fold.4 = (bf16[80,5120]{1,0:T(8,128)(2,1)}, f32[1,128]{1,0:T(1,128)}, f32[1,5120]{1,0:T(1,128)}) custom-call(f32[1]{0:T(128)S(6)} %copy.17.weight_ref, s32[2]{0:T(128)} %get-tuple-element.37.span_ref, bf16[640,128]{1,0:T(8,128)(2,1)} %all_gather.6.proj_ref, bf16[640,384]{1,0:T(8,128)(2,1)} %concatenate.24.picked_ref, ...), custom_call_target="tpu_custom_call" | custom-call | flops 1677721600 | bytes 13107200 | tf_op jit(solution)/shard_map/fold/pallas_call | solution.py:270
  108.9 0.8 constant_dynamic-slice_fusion.2
  109.7 0.1 pad_maximum_fusion.1
  109.8 1.4 collective-permute-start.4
  111.3 0.7 slice_bitcast_fusion.3
  111.9 0.1 pad_maximum_fusion
  112.0 1.2 collective-permute-start.3
  113.2 1.7 %collective-permute-start = (bf16[80,5120]{1,0:T(8,128)(2,1)}, bf16[80,5120]{1,0:T(8,128)(2,1)S(1)}, u32[]{:S(2)}, u32[]{:S(2)}) collective-permute-start(bf16[80,5120]{1,0:T(8,128)(2,1)} %get-tuple-element.12), channel_id=1, source_target_pairs={{0,18},{1,19},{2,16},{3,17},{4,22},{5,23},{6,20},{7,21},{8,26},{9,... | collective-permute-start | bytes 2457608 | tf_op jit(solution)/shard_map/ppermute | solution.py:335
  114.9 0.6 collective-permute-start.1
  115.5 1.1 concatenate.26.picked_ref
  116.6 11.2 %fold.6 = (bf16[80,5120]{1,0:T(8,128)(2,1)}, f32[1,128]{1,0:T(1,128)}) custom-call(f32[1]{0:T(128)S(6)} %copy.17.weight_ref, s32[2]{0:T(128)} %get-tuple-element.39.span_ref, bf16[640,128]{1,0:T(8,128)(2,1)} %all_gather.6.proj_ref, bf16[640,384]{1,0:T(8,128)(2,1)} %concatenate.26.picked_ref, bf16[128,128]{1,0:T(8,128)(2,1)} %constant.132.clone.perm_ref, ...), custom_call_target="tpu_custom_call" | custom-call | flops 1677721600 | bytes 13107200 | tf_op jit(solution)/shard_map/fold/pallas_call | solution.py:270
  127.8 1.2 collective-permute-start.2
  129.0 1.1 concatenate.27.picked_ref
  130.1 11.2 %fold.7 = (bf16[80,5120]{1,0:T(8,128)(2,1)}, f32[1,128]{1,0:T(1,128)}) custom-call(f32[1]{0:T(128)S(6)} %copy.17.weight_ref, s32[2]{0:T(128)} %get-tuple-element.40.span_ref, bf16[640,128]{1,0:T(8,128)(2,1)} %all_gather.6.proj_ref, bf16[640,384]{1,0:T(8,128)(2,1)} %concatenate.27.picked_ref, bf16[128,128]{1,0:T(8,128)(2,1)} %constant.132.clone.perm_ref, ...), custom_call_target="tpu_custom_call" | custom-call | flops 1677721600 | bytes 13107200 | tf_op jit(solution)/shard_map/fold/pallas_call | solution.py:270
  141.3 0.0 copy-done.1
  141.3 0.1 pad_maximum_fusion.2
  141.4 0.0 collective-permute-done.4
  141.4 0.9 collective-permute-start.5
  142.3 0.7 slice_bitcast_fusion
  142.9 0.0 collective-permute-done.3
  142.9 9.0 %collective-permute-done.5 = f32[240]{0:T(256)S(1)} collective-permute-done((f32[240]{0:T(256)S(1)}, f32[240]{0:T(256)S(1)}, u32[]{:S(2)}, u32[]{:S(2)}) %collective-permute-start.5) | collective-permute-done | bytes 992 | tf_op jit(solution)/shard_map/ppermute | solution.py:336
  151.9 0.1 maximum_add_fusion
  152.0 0.6 slice.23
  152.6 0.0 collective-permute-done
  152.6 0.0 collective-permute-done.1
  152.6 0.0 collective-permute-done.2
  152.6 2.7 %convert_add_fusion = f32[80,5120]{1,0:T(8,128)} fusion(bf16[80,5120]{1,0:T(8,128)(2,1)} %get-tuple-element.15, bf16[80,5120]{1,0:T(8,128)(2,1)S(1)} %collective-permute-done.2, bf16[80,5120]{1,0:T(8,128)(2,1)S(1)} %collective-permute-done.1, bf16[80,5120]{1,0:T(8,128)(2,1)S(1)} %collective-permute-done), kind=kLoop, calls=%fused_computation | loop fusion | flops 2867200 | bytes 4915200 | tf_op jit(solution)/shard_map/add | solution.py:339
  155.3 0.0 copy-done
  (4 shorter events, 0.0 us)
Async XLA Ops:
  7.2 73.4 %all-gather.2.cloned.1.call-start = ((), (), s32[]{:S(2)}) async-start(), calls=%async_computation | async-start | bytes 7372800 | tf_op jit(solution)/shard_map/all_gather | solution.py:195
  109.8 31.6 %collective-permute-start.4 = (f32[240]{0:T(256)S(1)}, f32[240]{0:T(256)S(1)}, u32[]{:S(2)}, u32[]{:S(2)}) collective-permute-start(f32[240]{0:T(256)S(1)} %pad_maximum_fusion.1), channel_id=1, source_target_pairs={{0,2},{1,3},{2,0},{3,1},{4,6},{5,7},{6,4},{7,5},{8,10},{9,11},{10,... | collective-permute-start | bytes 2888 | tf_op jit(solution)/shard_map/ppermute | solution.py:336
  112.0 30.9 %collective-permute-start.3 = (f32[240]{0:T(256)S(1)}, f32[240]{0:T(256)S(1)}, u32[]{:S(2)}, u32[]{:S(2)}) collective-permute-start(f32[240]{0:T(256)S(1)} %pad_maximum_fusion), channel_id=1, source_target_pairs={{0,18},{1,19},{2,16},{3,17},{4,22},{5,23},{6,20},{7,21},{8,26},{9,... | collective-permute-start | bytes 2888 | tf_op jit(solution)/shard_map/ppermute | solution.py:336
  113.2 39.3 %collective-permute-start = (bf16[80,5120]{1,0:T(8,128)(2,1)}, bf16[80,5120]{1,0:T(8,128)(2,1)S(1)}, u32[]{:S(2)}, u32[]{:S(2)}) collective-permute-start(bf16[80,5120]{1,0:T(8,128)(2,1)} %get-tuple-element.12), channel_id=1, source_target_pairs={{0,18},{1,19},{2,16},{3,17},{4,22},{5,23},{6,20},{7,21},{8,26},{9,... | collective-permute-start | bytes 2457608 | tf_op jit(solution)/shard_map/ppermute | solution.py:335
  114.9 37.6 %collective-permute-start.1 = (bf16[80,5120]{1,0:T(8,128)(2,1)}, bf16[80,5120]{1,0:T(8,128)(2,1)S(1)}, u32[]{:S(2)}, u32[]{:S(2)}) collective-permute-start(bf16[80,5120]{1,0:T(8,128)(2,1)} %get-tuple-element.13), channel_id=1, source_target_pairs={{0,2},{1,3},{2,0},{3,1},{4,6},{5,7},{6,4},{7,5},{8,10},{9,11},{10,... | collective-permute-start | bytes 2457608 | tf_op jit(solution)/shard_map/ppermute | solution.py:335
  127.8 24.7 %collective-permute-start.2 = (bf16[80,5120]{1,0:T(8,128)(2,1)}, bf16[80,5120]{1,0:T(8,128)(2,1)S(1)}, u32[]{:S(2)}, u32[]{:S(2)}) collective-permute-start(bf16[80,5120]{1,0:T(8,128)(2,1)} %get-tuple-element.14), channel_id=1, source_target_pairs={{0,16},{1,17},{2,18},{3,19},{4,20},{5,21},{6,22},{7,23},{8,24},{9,... | collective-permute-start | bytes 2457608 | tf_op jit(solution)/shard_map/ppermute | solution.py:335
  130.1 11.2 %copy-start.1 = (f32[1,128]{1,0:T(1,128)S(1)}, f32[1,128]{1,0:T(1,128)}, u32[]{:S(2)}) copy-start(f32[1,128]{1,0:T(1,128)} %get-tuple-element.19) | copy-start | bytes 1540
  141.4 10.5 %collective-permute-start.5 = (f32[240]{0:T(256)S(1)}, f32[240]{0:T(256)S(1)}, u32[]{:S(2)}, u32[]{:S(2)}) collective-permute-start(f32[240]{0:T(256)S(1)} %pad_maximum_fusion.2), channel_id=1, source_target_pairs={{0,16},{1,17},{2,18},{3,19},{4,20},{5,21},{6,22},{7,23},{8,24},{9,... | collective-permute-start | bytes 2888 | tf_op jit(solution)/shard_map/ppermute | solution.py:336
  152.0 3.3 %copy-start = (f32[240]{0:T(256)}, f32[240]{0:T(256)S(1)}, u32[]{:S(2)}) copy-start(f32[240]{0:T(256)S(1)} %maximum_add_fusion) | copy-start | bytes 2884
Sparse Core Ops, SparseCore 0:
  9.6 70.8 all-gather.1

commit v3 on v2

--- a/solution.py
+++ b/solution.py
@@ -223,8 +223,8 @@
     proj_all = gathered(proj)
 
     shifts = [(dm, dy) for dm in range(groups) for dy in range(mid)]
-    shifts.sort(key=lambda shift: -(shift[0] > 0) - (shift[1] > 0))
-    per_call = max(1, len(shifts) // 4)
+    shifts.sort(key=lambda shift: (shift[0] == 0, shift[1] == 0))
+    per_call = max(1, len(shifts) // 2)
     out_rows = per_call * final_rows
     width = rounded_up(out_rows + 1, LANES)
     place = np.arange(out_rows)

time: 163 us -> 156 us (0.957)
  Pallas kernels: 57.4 us -> 37.1 us
  local copies, waits for them, and re-layouts: 15.8 us -> 22.2 us
  waiting for transfers between devices: 42.4 us -> 48.3 us
    pallas_call x4 -> x2, Pallas kernels: 45.1 us -> 24.9 us  [fold_call(): pl.pallas_call(functools.partial(fold_kernel, block_rows, width, with_rig...]
    ppermute x3, waiting for transfers between devices: 8.96 us -> 17.9 us  [on_device(): vector = lax.ppermute(vector, ('mission', 'arc'), ring(dm, dy))]
    all_gather x1, waiting for transfers between devices: 32.8 us -> 29.8 us  [gathered(): lax.all_gather(array, 'arc', axis=0, tiled=True, axis_index_groups=gather...]
    slice x0 -> x2, local copies, waits for them, and re-layouts: none -> 2.82 us  [on_device(): block = fold[rows]]
    add x4 -> x2, other arithmetic: 2.47 us -> 0.14 us  [fold_call(): starts[:, None] + jnp.arange(final_rows, dtype=jnp.int32)[None, :]]
    concatenate x4 -> x2, local copies, waits for them, and re-layouts: 4.45 us -> 6.62 us  [fold_call(): jnp.concatenate(picked(lambda block: block * final_rows) + picked(lambda...]
  transfers between devices with their start and end apart: 7 -> 7, of which waited for: 2 -> 3; matrix products, arithmetic and copies ran while one was open for 8% -> 11% of each run, Pallas kernels for 21% -> 16%
where the time goes in v3:
time: 156 us; the launch traced here: 155 us
  waiting for transfers between devices  48.3 us (31%)
  Pallas kernels  37.1 us (24%)
  local copies, waits for them, and re-layouts  22.2 us (14%)
  blocking collectives  18.3 us (12%)
  between operations  16.3 us (10%)
  starting transfers between devices  7.15 us (5%)
  other arithmetic  5.23 us (3%)
    all_gather x1, waiting for transfers between devices, gathered(): lax.all_gather(array, 'arc', axis=0, tiled=True, axis_index_groups=gather...  29.8 us
    pallas_call x2, Pallas kernels, fold_call(): pl.pallas_call(functools.partial(fold_kernel, block_rows, width, with_rig...  24.9 us
    all_gather x1, blocking collectives, gathered(): lax.all_gather(array, 'arc', axis=0, tiled=True, axis_index_groups=gather...  18.3 us
    ppermute x3, waiting for transfers between devices, on_device(): vector = lax.ppermute(vector, ('mission', 'arc'), ring(dm, dy))  17.9 us
    pallas_call x1, Pallas kernels, on_device(): pl.pallas_call(projector_kernel, out_shape=jax.ShapeDtypeStruct((block_ro...  12.3 us
    concatenate x2, local copies, waits for them, and re-layouts, fold_call(): jnp.concatenate(picked(lambda block: block * final_rows) + picked(lambda...  6.62 us
    dynamic_slice x1, local copies, waits for them, and re-layouts, picked(): lax.dynamic_slice_in_dim(design_all, start_of(owner), final_rows, 1)  3.82 us
    ppermute x3, starting transfers between devices, on_device(): block = lax.ppermute(block, ('mission', 'arc'), ring(dm, dy))  3.62 us
  transfers between devices with their start and end apart: 7, of which 3 were waited for; matrix products, arithmetic and copies ran while one was open for 11% of the time, Pallas kernels for 16%

profile of v3, /device:TPU:0, one launch (start us, length us, event | category | flops | bytes accessed | tf_op | source)
XLA Modules:
  0.0 154.6 jit_solution(13097765995718346042)
XLA Ops:
  7.2 0.0 all-gather.2.cloned.1.call-start
  7.2 0.7 all-gather.2.cloned.1.call-update
  8.1 0.8 fusion
  8.9 0.1 iota_add_fusion.1
  8.9 0.8 add.278.rows_ref
  9.7 1.4 copy.15.arc_col_ref
  11.1 1.4 copy.16.kind_col_ref
  13.1 0.1 iota_add_fusion
  13.2 0.8 add.279.rows_ref
  15.3 1.2 pad_bitcast_fusion.1.arc_row_ref
  16.5 1.2 pad_bitcast_fusion.obs_row_ref
  17.7 12.3 %projector.1 = bf16[80,128]{1,0:T(8,128)(2,1)} custom-call(s32[2]{0:T(128)} %sizes_ref.1, f32[8]{0:T(128)} %kinds_ref.1, bf16[80,128]{1,0:T(8,128)(2,1)} %nuis_ref.1, s32[80,1]{1,0:T(8,128)} %copy.15.arc_col_ref, s32[1,128]{1,0:T(1,128)} %pad_bitcast_fusion.1.arc_row_ref, s32[80,1]{1,0:T(8,128)} %copy.16.kind_col_ref, f32[1,128]{1,0:T(1,128)} %pad_bitcast_fusion.obs_row_ref), custom_call_target="tpu_custom_call" | custom-call | flops 10000000 | bytes 100000 | tf_op jit(solution)/shard_map/projector/pallas_call | solution.py:207
  30.0 18.3 %all_gather.6.proj_ref = bf16[640,128]{1,0:T(8,128)(2,1)} all-gather(bf16[80,128]{1,0:T(8,128)(2,1)} %projector.1), channel_id=1, replica_groups={{0,1,4,5,8,9,12,13},{2,3,6,7,10,11,14,15},{16,17,20,21,24,25,28,29},{18..., dimensions={0}, use_global_device_ids=true | all-gather | bytes 184320 | tf_op jit(solution)/shard_map/all_gather | solution.py:195
  48.2 1.3 pad_add_fusion.span_ref
  49.5 1.2 pad_add_fusion.1.span_ref
  50.7 29.8 %all-gather.2.cloned.1.call-done.above_ref.mirror_ref = bf16[640,5120]{1,0:T(8,128)(2,1)} async-done(((bf16[80,5120]{1,0:T(8,128)(2,1)}), bf16[640,5120]{1,0:T(8,128)(2,1)}) %all-gather.2.cloned.1.call-update) | async-done | bytes 6553616 | tf_op jit(solution)/shard_map/all_gather | solution.py:195
  80.5 3.8 %constant_dynamic-slice_fusion.10 = (bf16[640,80]{1,0:T(8,128)(2,1)S(1)}, bf16[640,80]{1,0:T(8,128)(2,1)}, bf16[640,80]{1,0:T(8,128)(2,1)}, bf16[640,80]{1,0:T(8...) fusion(bf16[640,5120]{1,0:T(8,128)(2,1)} %all-gather.2.cloned.1, ...), kind=kLoop, calls=%fused_computation.11 | loop fusion | bytes 2457648 | tf_op jit(solution)/shard_map/dynamic_slice | solution.py:242
  84.3 3.3 %concatenate.26.picked_ref = bf16[640,768]{1,0:T(8,128)(2,1)} concatenate(bf16[640,80]{1,0:T(8,128)(2,1)S(1)} %get-tuple-element.30, bf16[640,80]{1,0:T(8,128)(2,1)S(1)} %get-tuple-element.29, bf16[640,96]{1,0:T(8,128)(2,1)S(1)} %broadcast.35, bf16[640,80]{1,0:T(8,128)(2,1)S(1)} %get-tuple-element.28, bf16[640,80]{1,0:T(8,128)(2,1)S(1)} %get-tuple-element.27, ...), dimensions={1} | concatenate | bytes 1966080 | tf_op jit(solution)/shard_map/concatenate | solution.py:248
  87.7 12.6 %fold.2 = (bf16[160,5120]{1,0:T(8,128)(2,1)}, f32[1,256]{1,0:T(1,128)}, f32[1,5120]{1,0:T(1,128)}) custom-call(f32[1]{0:T(128)S(6)} %copy.19.weight_ref, s32[2]{0:T(128)} %pad_add_fusion.span_ref, bf16[640,128]{1,0:T(8,128)(2,1)} %all_gather.6.proj_ref, bf16[640,768]{1,0:T(8,128)(2,1)} %concatenate.26.picked_ref, bf16[256,256]{1,0:T(8,128)(2,1)} %constant.126.clone.perm_ref, ...), custom_call_target="tpu_custom_call" | custom-call | flops 3355443200 | bytes 13107200 | tf_op jit(solution)/shard_map/fold/pallas_call | solution.py:270
  100.2 0.8 slice_bitcast_fusion.2
  101.0 1.5 fusion.2
  102.5 2.1 %collective-permute-start = (bf16[80,5120]{1,0:T(8,128)(2,1)S(1)}, bf16[80,5120]{1,0:T(8,128)(2,1)S(1)}, u32[]{:S(2)}, u32[]{:S(2)}) collective-permute-start(bf16[80,5120]{1,0:T(8,128)(2,1)S(1)} %get-tuple-element.31), channel_id=1, source_target_pairs={{0,18},{1,19},{2,16},{3,17},{4,22},{5,23},{6,20},{7,21},{8,26},{9,... | collective-permute-start | bytes 2457608 | tf_op jit(solution)/shard_map/ppermute | solution.py:335
  104.7 0.9 collective-permute-start.1
  105.6 3.3 %concatenate.27.picked_ref = bf16[640,768]{1,0:T(8,128)(2,1)} concatenate(bf16[640,80]{1,0:T(8,128)(2,1)} %get-tuple-element.25, bf16[640,80]{1,0:T(8,128)(2,1)} %get-tuple-element.24, bf16[640,96]{1,0:T(8,128)(2,1)S(1)} %broadcast.35, bf16[640,80]{1,0:T(8,128)(2,1)} %get-tuple-element.23, bf16[640,80]{1,0:T(8,128)(2,1)} %get-tuple-element.22, bf16[640,96]{1,0:T(8,128)(2,1)S(1)} %broadcast.35, ...), dimensions={1} | concatenate | bytes 1966080 | tf_op jit(solution)/shard_map/concatenate | solution.py:248
  108.8 12.3 %fold.3 = (bf16[160,5120]{1,0:T(8,128)(2,1)}, f32[1,256]{1,0:T(1,128)}) custom-call(f32[1]{0:T(128)S(6)} %copy.19.weight_ref, s32[2]{0:T(128)} %pad_add_fusion.1.span_ref, bf16[640,128]{1,0:T(8,128)(2,1)} %all_gather.6.proj_ref, bf16[640,768]{1,0:T(8,128)(2,1)} %concatenate.27.picked_ref, bf16[256,256]{1,0:T(8,128)(2,1)} %constant.126.clone.perm_ref, ...), custom_call_target="tpu_custom_call" | custom-call | flops 3355443200 | bytes 13107200 | tf_op jit(solution)/shard_map/fold/pallas_call | solution.py:270
  121.1 0.0 copy-start.1
  121.1 1.3 slice.32
  122.4 0.6 collective-permute-start.2
  123.0 0.8 constant_dynamic-slice_fusion.2
  123.9 0.1 pad_maximum_fusion.1
  123.9 1.1 collective-permute-start.4
  125.1 0.1 pad_maximum_fusion
  125.1 1.8 %collective-permute-start.3 = (f32[240]{0:T(256)S(1)}, f32[240]{0:T(256)S(1)}, u32[]{:S(2)}, u32[]{:S(2)}) collective-permute-start(f32[240]{0:T(256)S(1)} %pad_maximum_fusion), channel_id=1, source_target_pairs={{0,18},{1,19},{2,16},{3,17},{4,22},{5,23},{6,20},{7,21},{8,26},{9,... | collective-permute-start | bytes 2888 | tf_op jit(solution)/shard_map/ppermute | solution.py:336
  126.9 0.0 copy-done.1
  127.0 0.1 slice_bitcast_fusion.1
  127.0 0.1 pad_maximum_fusion.2
  127.1 14.9 %collective-permute-done.4 = f32[240]{0:T(256)S(1)} collective-permute-done((f32[240]{0:T(256)S(1)}, f32[240]{0:T(256)S(1)}, u32[]{:S(2)}, u32[]{:S(2)}) %collective-permute-start.4) | collective-permute-done | bytes 992 | tf_op jit(solution)/shard_map/ppermute | solution.py:336
  142.0 0.6 collective-permute-start.5
  142.5 0.0 collective-permute-done.3
  142.5 3.0 %collective-permute-done.5 = f32[240]{0:T(256)S(1)} collective-permute-done((f32[240]{0:T(256)S(1)}, f32[240]{0:T(256)S(1)}, u32[]{:S(2)}, u32[]{:S(2)}) %collective-permute-start.5) | collective-permute-done | bytes 992 | tf_op jit(solution)/shard_map/ppermute | solution.py:336
  145.5 0.1 maximum_add_fusion
  145.6 0.6 slice.39
  146.2 0.0 collective-permute-done
  146.2 0.0 collective-permute-done.1
  146.2 0.0 collective-permute-done.2
  146.2 0.0 copy-done
  146.2 1.5 convert_add_fusion
  147.8 0.0 copy-done.2
  (3 shorter events, 0.0 us)
Async XLA Ops:
  7.2 73.3 %all-gather.2.cloned.1.call-start = ((), (), s32[]{:S(2)}) async-start(), calls=%async_computation | async-start | bytes 7372800 | tf_op jit(solution)/shard_map/all_gather | solution.py:195
  102.5 43.6 %collective-permute-start = (bf16[80,5120]{1,0:T(8,128)(2,1)S(1)}, bf16[80,5120]{1,0:T(8,128)(2,1)S(1)}, u32[]{:S(2)}, u32[]{:S(2)}) collective-permute-start(bf16[80,5120]{1,0:T(8,128)(2,1)S(1)} %get-tuple-element.31), channel_id=1, source_target_pairs={{0,18},{1,19},{2,16},{3,17},{4,22},{5,23},{6,20},{7,21},{8,26},{9,... | collective-permute-start | bytes 2457608 | tf_op jit(solution)/shard_map/ppermute | solution.py:335
  104.7 41.5 %collective-permute-start.1 = (bf16[80,5120]{1,0:T(8,128)(2,1)S(1)}, bf16[80,5120]{1,0:T(8,128)(2,1)S(1)}, u32[]{:S(2)}, u32[]{:S(2)}) collective-permute-start(bf16[80,5120]{1,0:T(8,128)(2,1)S(1)} %get-tuple-element.32), channel_id=1, source_target_pairs={{0,16},{1,17},{2,18},{3,19},{4,20},{5,21},{6,22},{7,23},{8,24},{9,... | collective-permute-start | bytes 2457608 | tf_op jit(solution)/shard_map/ppermute | solution.py:335
  121.1 5.9 %copy-start.1 = (f32[1,256]{1,0:T(1,128)S(1)}, f32[1,256]{1,0:T(1,128)}, u32[]{:S(2)}) copy-start(f32[1,256]{1,0:T(1,128)} %get-tuple-element.12) | copy-start | bytes 3076
  121.1 25.1 %copy-start = (bf16[160,5120]{1,0:T(8,128)(2,1)S(1)}, bf16[160,5120]{1,0:T(8,128)(2,1)}, u32[]{:S(2)}) copy-start(bf16[160,5120]{1,0:T(8,128)(2,1)} %get-tuple-element.9) | copy-start | bytes 4915204
  122.4 23.8 %collective-permute-start.2 = (bf16[80,5120]{1,0:T(8,128)(2,1)S(1)}, bf16[80,5120]{1,0:T(8,128)(2,1)S(1)}, u32[]{:S(2)}, u32[]{:S(2)}) collective-permute-start(bf16[80,5120]{1,0:T(8,128)(2,1)S(1)} %slice.32), channel_id=1, source_target_pairs={{0,2},{1,3},{2,0},{3,1},{4,6},{5,7},{6,4},{7,5},{8,10},{9,11},{10,... | collective-permute-start | bytes 2457608 | tf_op jit(solution)/shard_map/ppermute | solution.py:335
  123.9 18.0 %collective-permute-start.4 = (f32[240]{0:T(256)S(1)}, f32[240]{0:T(256)S(1)}, u32[]{:S(2)}, u32[]{:S(2)}) collective-permute-start(f32[240]{0:T(256)S(1)} %pad_maximum_fusion.1), channel_id=1, source_target_pairs={{0,16},{1,17},{2,18},{3,19},{4,20},{5,21},{6,22},{7,23},{8,24},{9,... | collective-permute-start | bytes 2888 | tf_op jit(solution)/shard_map/ppermute | solution.py:336
  125.1 17.4 %collective-permute-start.3 = (f32[240]{0:T(256)S(1)}, f32[240]{0:T(256)S(1)}, u32[]{:S(2)}, u32[]{:S(2)}) collective-permute-start(f32[240]{0:T(256)S(1)} %pad_maximum_fusion), channel_id=1, source_target_pairs={{0,18},{1,19},{2,16},{3,17},{4,22},{5,23},{6,20},{7,21},{8,26},{9,... | collective-permute-start | bytes 2888 | tf_op jit(solution)/shard_map/ppermute | solution.py:336
  142.0 3.6 %collective-permute-start.5 = (f32[240]{0:T(256)S(1)}, f32[240]{0:T(256)S(1)}, u32[]{:S(2)}, u32[]{:S(2)}) collective-permute-start(f32[240]{0:T(256)S(1)} %pad_maximum_fusion.2), channel_id=1, source_target_pairs={{0,2},{1,3},{2,0},{3,1},{4,6},{5,7},{6,4},{7,5},{8,10},{9,11},{10,... | collective-permute-start | bytes 2888 | tf_op jit(solution)/shard_map/ppermute | solution.py:336
  145.6 2.2 %copy-start.2 = (f32[240]{0:T(256)}, f32[240]{0:T(256)S(1)}, u32[]{:S(2)}) copy-start(f32[240]{0:T(256)S(1)} %maximum_add_fusion) | copy-start | bytes 2884
Sparse Core Ops, SparseCore 0:
  9.6 70.7 all-gather.1
